TPU v7x, 128 devices: a whole 4x4x4 slice. The times are simulated.
128 devices in a mesh: ta: 16 (over z_hi, y, core), gx: 8 (over x, z_lo).
Axes of the slice: x: 4, y: 4, z: 4 (z_hi: 2, z_lo: 2; z = z_hi * 2 + z_lo), core: 2. Of those that a mesh axis runs over, the one named last changes fastest.
Arguments:
- eigenvectors: bfloat16 [16, 2, 32768, 3, 192], P('ta', None, 'gx'), may hold values from -6 to 6
- site_index: int32 [32768], P('gx'), may hold values from 0 to 32767, each once
- momenta: int32 [2, 3], replicated, may hold values from -3 to 3
- perambulators: bfloat16 [2, 16, 16, 768, 768], P(None, 'gx', 'ta'), may hold values from -6 to 6
- spin_perm: int32 [2, 4], replicated, may hold values from 0 to 3, each once within a row
- spin_sign: int32 [2, 4], replicated, may hold values from 0 to 1
Outputs:
- forward_box: bfloat16 [2, 16, 16, 768, 768], P(None, 'gx', 'ta')
- backward_box: bfloat16 [2, 16, 16, 768, 768], P(None, 'gx', 'ta')
Inputs may be any that keep to these rules, and one draw needn't show every extreme that they name: `site_index`: each lattice site appears exactly once. `spin_perm`: each row is a permutation of the spins.
All inputs are finite; a program needn't handle non-finite values.
Results may differ from a plain program's by a relative error of at most 0.008.
Values may be sent and summed in bfloat16 or wider, within the bound.
A program may use at most 128 MiB of HBM per device.

v0:
```python
import math

import jax
import jax.numpy as jnp
from jax import lax
from jax.sharding import PartitionSpec as P

L = 32
NEV = 192
COLOR = 3
SITES = 32768


def phases(site_index, momenta):
    first_coord = site_index // (L * L)
    second = site_index // L % L
    third_coord = site_index % L
    dotted = (
        momenta[:, 0:1] * first_coord[None, :]
        + momenta[:, 1:2] * second[None, :]
        + momenta[:, 2:3] * third_coord[None, :]
    )
    angles = jnp.mod(dotted, L).astype(jnp.float32) * (2.0 * math.pi / L)
    return (jnp.cos(angles), jnp.sin(angles))


def inner_rows(first_op, second_op):
    return lax.dot_general(
        first_op, second_op, (((0, 1), (0, 1)), ((), ())), preferred_element_type=jnp.float32
    )


def project(vectors, cosine, sine_value):
    real_part = vectors[0].astype(jnp.float32)
    imag_part = vectors[1].astype(jnp.float32)
    results = []
    for momentum in range(cosine.shape[0]):
        cosine_now = cosine[momentum][:, None, None]
        sine_now = sine_value[momentum][:, None, None]
        turned_real = (cosine_now * real_part - sine_now * imag_part).astype(jnp.bfloat16)
        turned_imag = (cosine_now * imag_part + sine_now * real_part).astype(jnp.bfloat16)
        real_out = inner_rows(vectors[0], turned_real) + inner_rows(vectors[1], turned_imag)
        imag_out = inner_rows(vectors[0], turned_imag) - inner_rows(vectors[1], turned_real)
        results.append(jnp.stack([real_out, imag_out]))
    return jnp.stack(results)


def spin_tables(spin_perm, spin_sign):
    spin_count = spin_perm.shape[1]
    matches = (
        spin_perm[:, :, None] == jnp.arange(spin_count, dtype=jnp.int32)[None, None, :]
    ).astype(jnp.float32)
    return matches * (2 * spin_sign - 1).astype(jnp.float32)[:, :, None]


def contract(form, first_op, second_op):
    return jnp.einsum(form, first_op, second_op, preferred_element_type=jnp.float32)


def complex_table(matrix):
    return jnp.stack([jnp.stack([matrix[0], -matrix[1]]), jnp.stack([matrix[1], matrix[0]])])


def pair_blocks(peram_block, sink_elems, source_elems, tables):
    spin_count = tables.shape[1]
    vector_count = sink_elems.shape[-1]
    dimension = spin_count * vector_count
    chiral = jnp.where(jnp.arange(spin_count) < spin_count // 2, 1.0, -1.0).astype(jnp.float32)
    blocks = peram_block.reshape(2, spin_count, vector_count, dimension)
    stacked = []
    for first_vertex, second_vertex in ((0, 1), (1, 0)):
        mixed_rows = contract(
            "rs,cslj->crlj", tables[first_vertex].astype(jnp.bfloat16), blocks
        ).astype(jnp.bfloat16)
        left_side = contract(
            "ockl,cslj->oskj", complex_table(sink_elems[first_vertex]), mixed_rows
        ).astype(jnp.bfloat16)
        left_side = left_side.reshape(2, dimension, spin_count, vector_count)
        signed = (tables[second_vertex] * chiral[None, :]).astype(jnp.bfloat16)
        turned = contract("cisk,sr->cirk", left_side, signed).astype(jnp.bfloat16)
        product = contract(
            "cisk,ockl->oisl", turned, complex_table(source_elems[second_vertex])
        ).astype(jnp.bfloat16)
        product = product.reshape(2, dimension, dimension)
        stacked.append(jnp.stack([product, jnp.stack([product[1], -product[0]])]))
    both_ways = jnp.stack(stacked)
    closed = contract("docim,cjm->doij", both_ways, peram_block)
    weights = jnp.repeat(chiral, vector_count) * (0.5 / math.sqrt(dimension))
    return (closed * weights).astype(jnp.bfloat16)


def on_device(eigenvectors, site_index, momenta, perambulators, spin_perm, spin_sign):
    cosine, sine_value = phases(site_index, momenta)
    partial_value = jnp.stack([project(eigenvectors[0], cosine, sine_value)])
    summed = lax.psum(partial_value, "gx")
    elementals = (summed * (0.5 / math.sqrt(COLOR * SITES * NEV))).astype(jnp.bfloat16)
    sink_count = perambulators.shape[1]
    all_elems = lax.all_gather(elementals, "ta", axis=0, tiled=True)
    sink_elems = lax.dynamic_slice_in_dim(
        all_elems, lax.axis_index("gx") * sink_count, sink_count, 0
    )
    tables = spin_tables(spin_perm, spin_sign)
    forward_rows = []
    backward_rows = []
    for sink_pos in range(sink_count):
        result = pair_blocks(
            perambulators[:, sink_pos, 0], sink_elems[sink_pos], elementals[0], tables
        )
        forward_cols = [result[0]]
        backward_cols = [result[1]]
        forward_rows.append(jnp.stack(forward_cols, 1))
        backward_rows.append(jnp.stack(backward_cols, 1))
    return (jnp.stack(forward_rows, 1), jnp.stack(backward_rows, 1))


def solution(mesh):
    return jax.shard_map(
        on_device,
        mesh=mesh,
        in_specs=(
            P("ta", None, "gx", None, None),
            P("gx"),
            P(),
            P(None, "gx", "ta", None, None),
            P(),
            P(),
        ),
        out_specs=(P(None, "gx", "ta", None, None), P(None, "gx", "ta", None, None)),
        check_vma=False,
    )
```

profile of v0, /device:TPU:7, one launch (start us, length us, event | category | flops | bytes accessed | tf_op | source)
XLA Modules:
  0.0 341.1 jit_solution(17740298056726697769)
XLA Ops:
  10.1 8.9 %fusion.119 = f32[192,192]{1,0:T(8,128)S(1)} fusion(f32[4096]{0:T(1024)S(1)} %bitcast.470, f32[4096]{0:T(1024)S(1)} %bitcast.474, bf16[1,2,4096,3,192]{2,4,3,1,0:T(8,128)(2,1)} %param.6), kind=kOutput, calls=%fused_computation.123 | convolution fusion | flops 920125440 | bytes 14336000 | tf_op jit(solution)/shard_map/dot_general | solution.py:28
  19.0 2.0 fusion.114
  21.0 2.0 fusion.109
  23.0 2.0 fusion.104
  25.0 2.0 fusion.149
  27.0 2.0 fusion.159
  29.0 2.4 fusion.169
  31.4 2.0 fusion.179
  34.5 71.8 %all-reduce.2.cloned.1.call-done = f32[1,2,2,192,192]{3,4,2,1,0:T(8,128)} async-done(((f32[1,2,2,192,192]{3,4,2,1,0:T(8,128)}), f32[1,2,2,192,192]{3,4,2,1,0:T(8,128)}) %all-reduce.2.cloned.1.call-update) | async-done | bytes 589840 | tf_op jit(solution)/shard_map/psum | solution.py:95
  108.8 2.7 fusion.248
  111.5 1.9 convert_bitcast_fusion.7
  113.4 3.4 convert_bitcast_fusion.5
  116.8 3.3 convert_bitcast_fusion.3
  120.1 3.3 convert_bitcast_fusion.1
  124.5 54.7 %all-gather.2.cloned.1.call-done = bf16[16,2,2,192,192]{4,3,2,1,0:T(8,128)(2,1)} async-done(((bf16[1,2,2,192,192]{4,3,2,1,0:T(8,128)(2,1)}), bf16[16,2,2,192,192]{4,3,2,1,0:T(8,128)(2,1)}) %all-gather.2.cloned.1.call-update) | async-done | bytes 4718608 | tf_op jit(solution)/shard_map/all_gather | solution.py:98
  179.1 1.9 fusion.242
  181.0 1.8 dynamic-slice_bitcast_fusion.7
  185.9 6.2 %reshape.233 = bf16[2,768,4,192]{3,2,1,0:T(4,128)(2,1)S(1)} reshape(bf16[2,4,192,768]{3,2,1,0:T(8,128)(2,1)} %copy.93) | data formatting | bytes 4718592 | tf_op jit(solution)/shard_map/reshape | solution.py:78
  192.1 4.9 %copy.95 = bf16[2,768,4,192]{1,2,3,0:T(4,128)(2,1)} copy(bf16[2,768,4,192]{3,2,1,0:T(4,128)(2,1)S(1)} %reshape.233) | data formatting | bytes 4718592 | tf_op jit(solution)/shard_map/reshape | solution.py:78
  197.0 3.2 convert_bitcast_fusion.6
  202.9 2.4 copy.97
  206.8 2.5 copy.99
  209.3 3.1 fusion.59
  214.0 6.1 %reshape.234 = bf16[2,768,4,192]{3,2,1,0:T(4,128)(2,1)S(1)} reshape(bf16[2,4,192,768]{3,2,1,0:T(8,128)(2,1)} %copy.102) | data formatting | bytes 4718592 | tf_op jit(solution)/shard_map/reshape | solution.py:78
  220.1 5.0 %copy.104 = bf16[2,768,4,192]{1,2,3,0:T(4,128)(2,1)} copy(bf16[2,768,4,192]{3,2,1,0:T(4,128)(2,1)S(1)} %reshape.234) | data formatting | bytes 4718592 | tf_op jit(solution)/shard_map/reshape | solution.py:78
  225.1 3.2 convert_bitcast_fusion.4
  231.4 2.5 copy.106
  233.8 2.4 copy.107
  236.3 2.6 copy.108
  238.9 1.6 maximum_bitcast_fusion.4
  245.7 7.9 %fusion.17 = bf16[2,2,768,768]{3,2,1,0:T(8,128)(2,1)S(1)} fusion(f32[768]{0:T(1024)S(1)} %mul.251, bf16[1,2,2,768,768]{4,3,2,1,0:T(8,128)(2,1)S(1)} %maximum_bitcast_fusion.1, bf16[1,2,2,768,768]{4,3,2,1,0:T(8,128)(2,1)S(1)} %maximum_bitcast_fusion, bf16[2,2,1,768,768]{4,3,2,1,0:T(8,128)(2,1)S(1)} %bitcast.451), kind=kOutput, calls=%fused_computation.27 | convolution fusion | flops 7257194496 | bytes 16519168 | tf_op jit(solution)/shard_map/docim,cjm->doij/dot_general | solution.py:57
  253.7 2.5 slice_bitcast_fusion.1
  259.7 6.1 %reshape.235 = bf16[2,768,4,192]{3,2,1,0:T(4,128)(2,1)S(1)} reshape(bf16[2,4,192,768]{3,2,1,0:T(8,128)(2,1)} %copy.112) | data formatting | bytes 4718592 | tf_op jit(solution)/shard_map/reshape | solution.py:78
  265.8 4.8 %copy.114 = bf16[2,768,4,192]{1,2,3,0:T(4,128)(2,1)} copy(bf16[2,768,4,192]{3,2,1,0:T(4,128)(2,1)S(1)} %reshape.235) | data formatting | bytes 4718592 | tf_op jit(solution)/shard_map/reshape | solution.py:78
  270.6 3.2 convert_bitcast_fusion.2
  276.4 2.4 copy.116
  280.3 2.7 copy.118
  283.0 3.1 fusion.61
  287.7 6.1 %reshape.236 = bf16[2,768,4,192]{3,2,1,0:T(4,128)(2,1)S(1)} reshape(bf16[2,4,192,768]{3,2,1,0:T(8,128)(2,1)} %copy.121) | data formatting | bytes 4718592 | tf_op jit(solution)/shard_map/reshape | solution.py:78
  293.8 4.8 %copy.123 = bf16[2,768,4,192]{1,2,3,0:T(4,128)(2,1)} copy(bf16[2,768,4,192]{3,2,1,0:T(4,128)(2,1)S(1)} %reshape.236) | data formatting | bytes 4718592 | tf_op jit(solution)/shard_map/reshape | solution.py:78
  298.6 3.2 convert_bitcast_fusion
  304.8 2.5 copy.125
  307.3 2.4 copy.126
  309.7 2.4 copy.127
  312.2 1.6 maximum_bitcast_fusion.6
  318.2 7.9 %fusion.16 = bf16[2,2,768,768]{3,2,1,0:T(8,128)(2,1)S(1)} fusion(f32[768]{0:T(1024)S(1)} %mul.251, bf16[1,2,2,768,768]{4,3,2,1,0:T(8,128)(2,1)S(1)} %maximum_bitcast_fusion.3, bf16[1,2,2,768,768]{4,3,2,1,0:T(8,128)(2,1)S(1)} %maximum_bitcast_fusion.2, bf16[2,2,1,768,768]{4,3,2,1,0:T(8,128)(2,1)S(1)} %bitcast.453), kind=kOutput, calls=%fused_computation.25 | convolution fusion | flops 7257194496 | bytes 16519168 | tf_op jit(solution)/shard_map/docim,cjm->doij/dot_general | solution.py:57
  328.3 2.5 copy.129
  331.3 2.5 copy.128
  (134 shorter events, 43.7 us)
Async XLA Ops:
  7.2 99.2 %all-reduce.2.cloned.1.call-start = ((), (), s32[]{:S(2)}) async-start(), calls=%async_computation | async-start | bytes 1572864 | tf_op jit(solution)/shard_map/psum | solution.py:95
  9.0 10.0 %slice-start.4 = ((s8[9437184]{0:T(1024)(128)(4,1)}), s8[4194304]{0:T(1024)(128)(4,1)S(1)}, s32[]{:S(2)}) async-start(s8[9437184]{0:T(1024)(128)(4,1)} %bitcast.478), calls=%async_computation.6 | async-start | bytes 8388608
  10.1 8.9 %slice-start.5 = ((s8[9437184]{0:T(1024)(128)(4,1)}), s8[4194304]{0:T(1024)(128)(4,1)S(1)}, s32[]{:S(2)}) async-start(s8[9437184]{0:T(1024)(128)(4,1)} %bitcast.478), calls=%async_computation.7 | async-start | bytes 8388608
  10.1 8.9 %slice-start.6 = ((s8[9437184]{0:T(1024)(128)(4,1)}), s8[1048576]{0:T(1024)(128)(4,1)S(1)}, s32[]{:S(2)}) async-start(s8[9437184]{0:T(1024)(128)(4,1)} %bitcast.478), calls=%async_computation.8 | async-start | bytes 2097152
  33.4 75.3 %copy-start.30 = (s32[2,4]{1,0:T(2,128)S(1)}, s32[2,4]{1,0:T(2,128)}, u32[]{:S(2)}) copy-start(s32[2,4]{1,0:T(2,128)} %param.11) | copy-start | bytes 100
  33.4 75.3 %copy-start.31 = (s32[2,4]{1,0:T(2,128)S(1)}, s32[2,4]{1,0:T(2,128)}, u32[]{:S(2)}) copy-start(s32[2,4]{1,0:T(2,128)} %param.10) | copy-start | bytes 100
  34.5 144.7 %all-gather.2.cloned.1.call-start = ((), (), s32[]{:S(2)}) async-start(), calls=%async_computation.1 | async-start | bytes 6684672 | tf_op jit(solution)/shard_map/all_gather | solution.py:98
  123.6 76.6 %copy-start.26 = (bf16[1,2,192,192]{2,3,1,0:T(8,128)(2,1)}, bf16[1,2,192,192]{2,3,1,0:T(8,128)(2,1)S(1)}, u32[]{:S(2)}) copy-start(bf16[1,2,192,192]{2,3,1,0:T(8,128)(2,1)S(1)} %get-tuple-element.57) | copy-start | bytes 442372
  123.6 76.6 %copy-start.28 = (bf16[1,2,192,192]{2,3,1,0:T(8,128)(2,1)}, bf16[1,2,192,192]{2,3,1,0:T(8,128)(2,1)S(1)}, u32[]{:S(2)}) copy-start(bf16[1,2,192,192]{2,3,1,0:T(8,128)(2,1)S(1)} %get-tuple-element.58) | copy-start | bytes 442372
  206.8 2.5 copy-start.17
  206.8 2.5 copy-start.18
  206.8 2.5 copy-start.21
  220.1 8.2 %copy-start.22 = (bf16[1,2,192,192]{2,3,1,0:T(8,128)(2,1)S(1)}, bf16[1,2,192,192]{2,3,1,0:T(8,128)(2,1)}, u32[]{:S(2)}) copy-start(bf16[1,2,192,192]{2,3,1,0:T(8,128)(2,1)} %get-tuple-element.61) | copy-start | bytes 442372
  220.1 8.2 %copy-start.24 = (bf16[1,2,192,192]{2,3,1,0:T(8,128)(2,1)S(1)}, bf16[1,2,192,192]{2,3,1,0:T(8,128)(2,1)}, u32[]{:S(2)}) copy-start(bf16[1,2,192,192]{2,3,1,0:T(8,128)(2,1)} %get-tuple-element.62) | copy-start | bytes 442372
  231.4 7.5 %copy-start.7 = (bf16[1,768,768]{2,1,0:T(8,128)(2,1)S(1)}, bf16[1,768,768]{2,1,0:T(8,128)(2,1)}, u32[]{:S(2)}) copy-start(bf16[1,768,768]{2,1,0:T(8,128)(2,1)} %copy.97) | copy-start | bytes 3538948
  238.9 2.0 copy-start.1
  240.9 1.3 copy-start.8
  240.9 1.6 copy-start.10
  242.5 1.7 copy-start.2
  242.5 2.9 slice-start
  244.2 1.5 slice-start.1
  253.6 2.5 copy-start.15
  253.6 2.5 copy-start.16
  253.6 2.5 copy-start.20
  253.7 3.0 copy-start.12
  265.8 8.0 %copy-start.27 = (bf16[1,2,192,192]{2,3,1,0:T(8,128)(2,1)S(1)}, bf16[1,2,192,192]{2,3,1,0:T(8,128)(2,1)}, u32[]{:S(2)}) copy-start(bf16[1,2,192,192]{2,3,1,0:T(8,128)(2,1)} %copy-done.26) | copy-start | bytes 442372
  265.8 8.0 %copy-start.29 = (bf16[1,2,192,192]{2,3,1,0:T(8,128)(2,1)S(1)}, bf16[1,2,192,192]{2,3,1,0:T(8,128)(2,1)}, u32[]{:S(2)}) copy-start(bf16[1,2,192,192]{2,3,1,0:T(8,128)(2,1)} %copy-done.28) | copy-start | bytes 442372
  280.2 2.7 copy-start.13
  280.2 2.7 copy-start.14
  280.3 2.7 copy-start.19
  293.8 8.0 %copy-start.23 = (bf16[1,2,192,192]{2,3,1,0:T(8,128)(2,1)S(1)}, bf16[1,2,192,192]{2,3,1,0:T(8,128)(2,1)}, u32[]{:S(2)}) copy-start(bf16[1,2,192,192]{2,3,1,0:T(8,128)(2,1)} %get-tuple-element.61) | copy-start | bytes 442372
  293.8 8.0 %copy-start.25 = (bf16[1,2,192,192]{2,3,1,0:T(8,128)(2,1)S(1)}, bf16[1,2,192,192]{2,3,1,0:T(8,128)(2,1)}, u32[]{:S(2)}) copy-start(bf16[1,2,192,192]{2,3,1,0:T(8,128)(2,1)} %get-tuple-element.62) | copy-start | bytes 442372
  304.8 7.3 %copy-start.6 = (bf16[1,768,768]{2,1,0:T(8,128)(2,1)S(1)}, bf16[1,768,768]{2,1,0:T(8,128)(2,1)}, u32[]{:S(2)}) copy-start(bf16[1,768,768]{2,1,0:T(8,128)(2,1)} %copy.116) | copy-start | bytes 3538948
  312.2 2.0 copy-start
  314.2 1.3 copy-start.9
  314.2 1.6 copy-start.11
  314.2 2.4 copy-start.3
  314.2 2.8 slice-start.2
  315.8 2.4 slice-start.3
  326.1 1.7 copy-start.5
  328.2 2.6 copy-start.4
Sparse Core Ops, SparseCore 0:
  34.6 71.6 all-reduce.1
  108.8 70.3 all-gather.1
where the time goes:
time: 346 us; the launch traced here: 341 us
  waiting for transfers between devices  127 us (37%)
  local copies, waits for them, and re-layouts  102 us (29%)
  matrix products  78.5 us (23%)
  other arithmetic  18.6 us (5%)
  between operations  15.2 us (4%)
    psum x1, waiting for transfers between devices, on_device(): summed = lax.psum(partial_value, 'gx')  71.8 us
    dot_general x18, matrix products, contract(): jnp.einsum(form, first_op, second_op, preferred_element_type=jnp.float32)  55.2 us
    all_gather x1, waiting for transfers between devices, on_device(): all_elems = lax.all_gather(elementals, 'ta', axis=0, tiled=True)  54.7 us
    reshape x8, local copies, waits for them, and re-layouts, pair_blocks(): left_side = left_side.reshape(2, dimension, spin_count, vector_count)  44 us
    dot_general x8, matrix products, inner_rows(): lax.dot_general(first_op, second_op, (((0, 1), (0, 1)), ((), ())), prefer...  23.2 us
    unnamed x80, local copies, waits for them, and re-layouts  14.4 us
    another operation x4, local copies, waits for them, and re-layouts, pair_blocks(): stacked.append(jnp.stack([product, jnp.stack([product[1], -product[0]])]))  10.2 us
    slice x4, local copies, waits for them, and re-layouts, pair_blocks(): stacked.append(jnp.stack([product, jnp.stack([product[1], -product[0]])]))  9.7 us
  transfers between devices with their start and end apart: 2, of which 2 were waited for; matrix products, arithmetic and copies ran while one was open for 5% of the time, Pallas kernels for 0%

commit v1 on v0

v1 whole, which is shorter than its diff:
```python
import functools
import math

import jax
import jax.numpy as jnp
from jax import lax
from jax.experimental import pallas as pl
from jax.experimental.pallas import tpu as pltpu
from jax.sharding import PartitionSpec as P

L = 32
NEV = 192
COLOR = 3
SPIN = 4
SITES = 32768
NDIM = SPIN * NEV
PAIR = 2 * NEV
MESH = pl.DeviceIdType.MESH
F32 = jnp.float32
BF16 = jnp.bfloat16
NT = (((1,), (1,)), ((), ()))
NN = (((1,), (0,)), ((), ()))


def dot(a, b, dims=NN):
    return lax.dot_general(a, b, dims, preferred_element_type=F32)


def project_kernel(chunk, mom_ref, site_ref, vec_ref, out_ref, acc_ref, turned_ref):
    step = pl.program_id(0)
    last = pl.num_programs(0) - 1

    @pl.when(step == 0)
    def _():
        acc_ref[...] = jnp.zeros_like(acc_ref)

    site = site_ref[...]
    first, second, third = site >> 10, (site >> 5) & (L - 1), site & (L - 1)
    real = vec_ref[0, 0].astype(F32)
    imag = vec_ref[1, 0].astype(F32)
    for p in range(2):
        dotted = mom_ref[p, 0] * first + mom_ref[p, 1] * second + mom_ref[p, 2] * third
        angle = (dotted & (L - 1)).astype(F32) * (2.0 * math.pi / L)
        cosine, sine = jnp.cos(angle), jnp.sin(angle)
        turned_ref[p * NEV : (p + 1) * NEV] = (cosine * real - sine * imag).astype(BF16)
        turned_ref[PAIR + p * NEV : PAIR + (p + 1) * NEV] = (cosine * imag + sine * real).astype(BF16)
    plain = jnp.concatenate([vec_ref[0, 0], vec_ref[1, 0]], axis=0)
    acc_ref[...] += dot(plain, turned_ref[...], NT)

    @pl.when(step == last)
    def _():
        norm = 0.5 / math.sqrt(COLOR * SITES * NEV)
        out_ref[0:NEV] = ((acc_ref[0:NEV, 0:PAIR] + acc_ref[NEV:PAIR, PAIR:NDIM]) * norm).astype(BF16)
        out_ref[NEV:PAIR] = ((acc_ref[0:NEV, PAIR:NDIM] - acc_ref[NEV:PAIR, 0:PAIR]) * norm).astype(BF16)


def project(vectors, site_index, momenta, chunk=1024, interpret=False):
    sites = vectors.shape[-1]
    cuts = sites // chunk
    return pl.pallas_call(
        functools.partial(project_kernel, chunk),
        out_shape=jax.ShapeDtypeStruct((PAIR, PAIR), BF16),
        grid=(COLOR * cuts,),
        in_specs=[
            pl.BlockSpec(memory_space=pltpu.SMEM),
            pl.BlockSpec((1, chunk), lambda i: (0, i % cuts)),
            pl.BlockSpec((2, 1, NEV, chunk), lambda i: (0, i // cuts, 0, i % cuts)),
        ],
        out_specs=pl.BlockSpec((PAIR, PAIR), lambda i: (0, 0)),
        scratch_shapes=[pltpu.VMEM((PAIR, NDIM), F32), pltpu.VMEM((NDIM, chunk), BF16)],
        compiler_params=pltpu.CompilerParams(
            dimension_semantics=("arbitrary",), vmem_limit_bytes=56 * 1024 * 1024
        ),
        cost_estimate=pl.CostEstimate(
            flops=2 * PAIR * NDIM * COLOR * sites, bytes_accessed=4 * NEV * COLOR * sites, transcendentals=0
        ),
        name="project",
        interpret=interpret,
    )(momenta, site_index, vectors)


def sum_kernel(count, part_ref, out_ref, held, send_sem, recv_sem, back_send, back_recv):
    me = lax.axis_index("gx")
    barrier = pltpu.get_barrier_semaphore()
    for hop in range(1, count):
        pl.semaphore_signal(
            barrier, inc=1, device_id={"gx": lax.rem(me + hop, count)}, device_id_type=MESH
        )
    pl.semaphore_wait(barrier, count - 1)
    copies = []
    for hop in range(1, count):
        peer = lax.rem(me + hop, count)
        copy = pltpu.make_async_remote_copy(
            src_ref=part_ref.at[peer],
            dst_ref=held.at[hop],
            send_sem=send_sem.at[hop],
            recv_sem=recv_sem.at[hop],
            device_id={"gx": peer},
            device_id_type=MESH,
        )
        copy.start()
        copies.append(copy)
    total = part_ref[me].astype(F32)
    for hop in range(1, count):
        copies[hop - 1].wait_recv()
        total = total + held[hop].astype(F32)
    out_ref[me] = total.astype(BF16)
    backs = []
    for hop in range(1, count):
        back = pltpu.make_async_remote_copy(
            src_ref=out_ref.at[me],
            dst_ref=out_ref.at[me],
            send_sem=back_send.at[hop],
            recv_sem=back_recv.at[hop],
            device_id={"gx": lax.rem(me + hop, count)},
            device_id_type=MESH,
        )
        back.start()
        backs.append(back)
    for hop in range(1, count):
        copies[hop - 1].wait_send()
        backs[hop - 1].wait()


def sum_over_sites(partial, count):
    rows = PAIR // count
    shape = (count, rows, PAIR)
    summed = pl.pallas_call(
        functools.partial(sum_kernel, count),
        out_shape=jax.ShapeDtypeStruct(shape, BF16),
        in_specs=[pl.BlockSpec(memory_space=pltpu.VMEM)],
        out_specs=pl.BlockSpec(memory_space=pltpu.VMEM),
        scratch_shapes=[pltpu.VMEM(shape, BF16)] + [pltpu.SemaphoreType.DMA((count,))] * 4,
        compiler_params=pltpu.CompilerParams(
            collective_id=0, has_side_effects=True, vmem_limit_bytes=8 * 1024 * 1024
        ),
        name="sum_over_sites",
    )(partial.reshape(shape))
    return summed.reshape(PAIR, PAIR)


def close_kernel(rows, perm_ref, sign_ref, elem_ref, tau_ref, out_ref, table, spins, turned, mixed):
    pair, block = pl.program_id(0), pl.program_id(1)

    @pl.when((pair == 0) & (block == 0))
    def _():
        table[0:NEV, 0:PAIR] = elem_ref[0:NEV]
        table[0:NEV, PAIR:NDIM] = elem_ref[NEV:PAIR]
        table[NEV:PAIR, 0:PAIR] = -elem_ref[NEV:PAIR]
        table[NEV:PAIR, PAIR:NDIM] = elem_ref[0:NEV]

    @pl.when(block == 0)
    def _():
        for a in range(SPIN):
            cut = slice(a * NEV, (a + 1) * NEV)
            spins[a, :, 0:NEV] = tau_ref[0, 0, 0, :, cut]
            spins[a, :, NEV:PAIR] = tau_ref[1, 0, 0, :, cut]
        for q in range(2):
            for a in range(SPIN):
                into = perm_ref[q, a]
                sign = (2 * sign_ref[q, a] - 1) * jnp.where(into < SPIN // 2, 1, -1)
                moved = spins[into] * sign.astype(F32).astype(BF16)
                turned[q, 0, :, a * NEV : (a + 1) * NEV] = moved[:, 0:NEV]
                turned[q, 1, :, a * NEV : (a + 1) * NEV] = moved[:, NEV:PAIR]

    start = pl.multiple_of(block * rows, rows)
    for a in range(SPIN):
        product = dot(spins[a, pl.ds(start, rows), :], table[...]).astype(BF16)
        for c in range(2):
            for q in range(2):
                left = c * PAIR + q * NEV
                mixed[q, c, :, a * NEV : (a + 1) * NEV] = product[:, left : left + NEV]
    for q in range(2):
        real, imag = mixed[q, 0], mixed[q, 1]
        out_ref[q, 0, 0] = (dot(real, turned[q, 0], NT) + dot(imag, turned[q, 1], NT)).astype(BF16)
        out_ref[q, 1, 0] = (dot(imag, turned[q, 0], NT) - dot(real, turned[q, 1], NT)).astype(BF16)


def close_pairs(peram, elem, spin_perm, spin_sign, rows=384, interpret=False):
    sinks = peram.shape[1]
    return pl.pallas_call(
        functools.partial(close_kernel, rows),
        out_shape=jax.ShapeDtypeStruct((2, 2, sinks, NDIM, NDIM), BF16),
        grid=(sinks, NDIM // rows),
        in_specs=[
            pl.BlockSpec(memory_space=pltpu.SMEM),
            pl.BlockSpec(memory_space=pltpu.SMEM),
            pl.BlockSpec((PAIR, PAIR), lambda i, j: (0, 0)),
            pl.BlockSpec((2, 1, 1, NDIM, NDIM), lambda i, j: (0, i, 0, 0, 0)),
        ],
        out_specs=pl.BlockSpec((2, 2, 1, rows, NDIM), lambda i, j: (0, 0, i, j, 0)),
        scratch_shapes=[
            pltpu.VMEM((PAIR, NDIM), BF16),
            pltpu.VMEM((SPIN, NDIM, PAIR), BF16),
            pltpu.VMEM((2, 2, NDIM, NDIM), BF16),
            pltpu.VMEM((2, 2, rows, NDIM), BF16),
        ],
        compiler_params=pltpu.CompilerParams(
            dimension_semantics=("arbitrary", "arbitrary"), vmem_limit_bytes=48 * 1024 * 1024
        ),
        cost_estimate=pl.CostEstimate(
            flops=sinks * (16 * NDIM**3 + 16 * NDIM * NDIM * NEV),
            bytes_accessed=sinks * 12 * NDIM * NDIM,
            transcendentals=0,
        ),
        name="close_pairs",
        interpret=interpret,
    )(spin_perm, spin_sign, elem, peram)


def apply_kernel(swap_ref, perm_ref, sign_ref, even_ref, odd_ref, x_ref, out0_ref, out1_ref, table):
    pair = pl.program_id(0)
    first = (pair == 0) == (swap_ref[0] == 0)
    elem = jnp.where(first, even_ref[...], odd_ref[...])
    chiral = jnp.where(lax.broadcasted_iota(jnp.int32, (1, NDIM), 1) < NDIM // 2, 1.0, -1.0)
    weights = chiral * (0.5 / math.sqrt(NDIM))
    for d in range(2):
        real = elem[0:NEV, d * NEV : (d + 1) * NEV]
        imag = elem[NEV:PAIR, d * NEV : (d + 1) * NEV]
        table[0:NEV, 0:NEV] = real
        table[0:NEV, NEV:PAIR] = -imag
        table[NEV:PAIR, 0:NEV] = imag
        table[NEV:PAIR, NEV:PAIR] = real
        out_ref = out0_ref if d == 0 else out1_ref
        for r in range(SPIN):
            start = pl.multiple_of(perm_ref[d, r] * NEV, NEV)
            sign = (2 * sign_ref[d, r] - 1).astype(F32)
            stacked = jnp.concatenate(
                [x_ref[1 - d, 0, 0, pl.ds(start, NEV), :], x_ref[1 - d, 1, 0, pl.ds(start, NEV), :]], axis=0
            )
            done = dot(table[...], stacked) * (weights * sign)
            out_ref[0, 0, 0, r * NEV : (r + 1) * NEV] = done[0:NEV].astype(BF16)
            out_ref[1, 0, 0, r * NEV : (r + 1) * NEV] = done[NEV:PAIR].astype(BF16)


def apply_sinks(swap, even, odd, blocks, spin_perm, spin_sign, interpret=False):
    sinks = blocks.shape[2]
    shape = jax.ShapeDtypeStruct((2, sinks, 1, NDIM, NDIM), BF16)
    out_spec = pl.BlockSpec((2, 1, 1, NDIM, NDIM), lambda i: (0, i, 0, 0, 0))
    smem = pl.BlockSpec(memory_space=pltpu.SMEM)
    whole = pl.BlockSpec((PAIR, PAIR), lambda i: (0, 0))
    return pl.pallas_call(
        apply_kernel,
        out_shape=(shape, shape),
        grid=(sinks,),
        in_specs=[
            smem,
            smem,
            smem,
            whole,
            whole,
            pl.BlockSpec((2, 2, 1, NDIM, NDIM), lambda i: (0, 0, i, 0, 0)),
        ],
        out_specs=(out_spec, out_spec),
        scratch_shapes=[pltpu.VMEM((PAIR, PAIR), BF16)],
        compiler_params=pltpu.CompilerParams(
            dimension_semantics=("arbitrary",), vmem_limit_bytes=48 * 1024 * 1024
        ),
        cost_estimate=pl.CostEstimate(
            flops=sinks * 16 * NDIM * NDIM * NEV, bytes_accessed=sinks * 16 * NDIM * NDIM, transcendentals=0
        ),
        name="apply_sinks",
        interpret=interpret,
    )(swap, spin_perm, spin_sign, even, odd, blocks)


def on_device(times, sites, eigenvectors, site_index, momenta, perambulators, spin_perm, spin_sign):
    vectors = jnp.transpose(eigenvectors[0], (0, 2, 3, 1))
    partial = project(vectors, site_index.reshape(1, -1), momenta)
    elem = sum_over_sites(partial, sites)
    sinks = times // sites
    moved = []
    for turn in range(sinks):
        route = []
        for t in range(times):
            for g in range(sites):
                target = g + sites * ((t + turn) % sinks)
                route.append((t * sites + g, target * sites + t // sinks))
        moved.append(lax.ppermute(elem, ("ta", "gx"), route))
    blocks = close_pairs(perambulators, elem, spin_perm, spin_sign)
    swap = (lax.axis_index("ta") // sites).astype(jnp.int32).reshape(1)
    return apply_sinks(swap, moved[0], moved[1], blocks, spin_perm, spin_sign)


def solution(mesh):
    return jax.shard_map(
        functools.partial(on_device, mesh.shape["ta"], mesh.shape["gx"]),
        mesh=mesh,
        in_specs=(
            P("ta", None, "gx", None, None),
            P("gx"),
            P(),
            P(None, "gx", "ta", None, None),
            P(),
            P(),
        ),
        out_specs=(P(None, "gx", "ta", None, None), P(None, "gx", "ta", None, None)),
        check_vma=False,
    )
```

time: 346 us -> 80.5 us (0.23)
  waiting for transfers between devices: 127 us -> 0.01 us
  local copies, waits for them, and re-layouts: 102 us -> 0.97 us
  matrix products: 78.5 us -> 0 us
  Pallas kernels: 0 us -> 64.6 us
  other arithmetic: 18.6 us -> 0 us
  between operations: 15.2 us -> 0.7 us
  starting transfers between devices: 0.08 us -> 12.7 us
    dot_general x26 -> x0, matrix products: 78.5 us -> none  [the longest x18 55.2 us: contract(): jnp.einsum(form, first_op, second_op, preferred_element_type=jnp.float32)]
    psum x1 -> x0, waiting for transfers between devices: 71.8 us -> none  [on_device(): summed = lax.psum(partial_value, 'gx')]
    pallas_call x0 -> x4, Pallas kernels: none -> 64.6 us  [the longest x1 28 us: close_pairs(): pl.pallas_call(functools.partial(close_kernel, rows), out_shape=jax.Shape...]
    all_gather x1 -> x0, waiting for transfers between devices: 54.7 us -> none  [on_device(): all_elems = lax.all_gather(elementals, 'ta', axis=0, tiled=True)]
    reshape x8 -> x0, local copies, waits for them, and re-layouts: 44 us -> none  [pair_blocks(): left_side = left_side.reshape(2, dimension, spin_count, vector_count)]
    slice x9 -> x0, local copies, waits for them, and re-layouts: 15.2 us -> none  [the longest x4 9.7 us: pair_blocks(): stacked.append(jnp.stack([product, jnp.stack([product[1], -product[0]])]))]
    unnamed x80 -> x8, local copies, waits for them, and re-layouts: 14.4 us -> 0.97 us
    another operation x6 -> x0, local copies, waits for them, and re-layouts: 12.9 us -> none  [the longest x4 10.2 us: pair_blocks(): stacked.append(jnp.stack([product, jnp.stack([product[1], -product[0]])]))]
  transfers between devices with their start and end apart: 2 -> 2, of which waited for: 2 -> 0; matrix products, arithmetic and copies ran while one was open for 5% -> 0% of each run, Pallas kernels for 0% -> 35%
where the time goes in v1:
time: 80.5 us; the launch traced here: 79 us
  Pallas kernels  64.6 us (80%)
  starting transfers between devices  12.7 us (16%)
  local copies, waits for them, and re-layouts  0.97 us (1%)
    pallas_call x1, Pallas kernels, close_pairs(): pl.pallas_call(functools.partial(close_kernel, rows), out_shape=jax.Shape...  28 us
    pallas_call x1, Pallas kernels, project(): pl.pallas_call(functools.partial(project_kernel, chunk), out_shape=jax.Sh...  14.8 us
    ppermute x2, starting transfers between devices, on_device(): moved.append(lax.ppermute(elem, ('ta', 'gx'), route))  12.7 us
    pallas_call x1, Pallas kernels, sum_over_sites(): pl.pallas_call(functools.partial(sum_kernel, count), out_shape=jax.ShapeD...  11.7 us
    pallas_call x1, Pallas kernels, apply_sinks(): pl.pallas_call(apply_kernel, out_shape=(shape, shape), grid=(sinks,), in_...  10 us
  transfers between devices with their start and end apart: 2, of which 0 were waited for; matrix products, arithmetic and copies ran while one was open for 0% of the time, Pallas kernels for 35%

profile of v1, /device:TPU:7, one launch (start us, length us, event | category | flops | bytes accessed | tf_op | source)
XLA Modules:
  0.0 79.0 jit_solution(7965766495630626900)
XLA Ops:
  0.6 0.0 copy-start.1
  0.6 0.0 copy-start.2
  0.7 0.0 copy-start.3
  0.7 14.8 %project.1 = bf16[384,384]{1,0:T(8,128)(2,1)} custom-call(s32[2,3]{1,0:T(2,128)} %mom_ref.1, s32[1,4096]{1,0:T(1,128)} %bitcast.12, bf16[2,3,192,4096]{3,2,1,0:T(8,128)(2,1)} %bitcast.11), custom_call_target="tpu_custom_call" | custom-call | flops 7247757312 | bytes 9437184 | tf_op jit(solution)/shard_map/project/pallas_call | solution.py:60
  15.5 0.0 copy-start
  15.5 1.0 %copy-done = bf16[384,384]{1,0:T(8,128)(2,1)S(1)} copy-done((bf16[384,384]{1,0:T(8,128)(2,1)S(1)}, bf16[384,384]{1,0:T(8,128)(2,1)}, u32[]{:S(2)}) %copy-start) | copy-done | bytes 294936
  16.5 11.7 %sum_over_sites.1 = bf16[8,48,384]{2,1,0:T(8,128)(2,1)S(1)} custom-call(bf16[8,48,384]{2,1,0:T(8,128)(2,1)S(1)} %bitcast.10), custom_call_target="tpu_custom_call" | custom-call | tf_op jit(solution)/shard_map/sum_over_sites/pallas_call | solution.py:128
  28.2 7.0 %collective-permute-start.1 = (bf16[384,384]{1,0:T(8,128)(2,1)S(1)}, bf16[384,384]{1,0:T(8,128)(2,1)S(1)}, u32[]{:S(2)}, u32[]{:S(2)}) collective-permute-start(bf16[384,384]{1,0:T(8,128)(2,1)S(1)} %bitcast.7), channel_id=1, source_target_pairs={{0,64},{1,72},{2,80},{3,88},{4,96},{5,104},{6,112},{7,120},{8,0},{... | collective-permute-start | bytes 884744 | tf_op jit(solution)/shard_map/ppermute | solution.py:279
  35.2 5.7 %collective-permute-start = (bf16[384,384]{1,0:T(8,128)(2,1)S(1)}, bf16[384,384]{1,0:T(8,128)(2,1)S(1)}, u32[]{:S(2)}, u32[]{:S(2)}) collective-permute-start(bf16[384,384]{1,0:T(8,128)(2,1)S(1)} %bitcast.8), channel_id=1, source_target_pairs={{0,0},{1,8},{2,16},{3,24},{4,32},{5,40},{6,48},{7,56},{8,64},{9,72... | collective-permute-start | bytes 884744 | tf_op jit(solution)/shard_map/ppermute | solution.py:279
  40.9 0.0 copy-done.1
  40.9 0.0 copy-done.2
  40.9 0.0 copy-done.3
  40.9 28.0 %close_pairs.1.x_ref = bf16[2,2,2,768,768]{4,3,2,1,0:T(8,128)(2,1)} custom-call(s32[2,4]{1,0:T(2,128)S(1)} %copy-done.2, s32[2,4]{1,0:T(2,128)S(1)} %copy-done.3, bf16[384,384]{1,0:T(8,128)(2,1)S(1)} %bitcast.9, bf16[2,2,1,768,768]{4,3,2,1,0:T(8,128)(2,1)S(1)} %copy-done.1), custom_call_target="tpu_custom_call" | custom-call | flops 18119393280 | bytes 14155776 | tf_op jit(solution)/shard_map/close_pairs/pallas_call | solution.py:181
  68.9 0.0 collective-permute-done.1.odd_ref
  68.9 0.0 collective-permute-done.even_ref
  69.0 10.0 %apply_sinks.1 = (bf16[2,2,1,768,768]{4,3,2,1,0:T(8,128)(2,1)}, bf16[2,2,1,768,768]{4,3,2,1,0:T(8,128)(2,1)}) custom-call(s32[1]{0:T(128)} %bitcast.swap_ref, s32[2,4]{1,0:T(2,128)S(1)} %copy-done.2, s32[2,4]{1,0:T(2,128)S(1)} %copy-done.3, bf16[384,384]{1,0:T(8,128)(2,1)S(1)} %collective-permute-done.even_ref, ...), custom_call_target="tpu_custom_call" | custom-call | flops 3623878656 | bytes 18874368 | tf_op jit(solution)/shard_map/apply_sinks/pallas_call | solution.py:242
Async XLA Ops:
  0.6 40.3 %copy-start.1 = (bf16[2,2,1,768,768]{4,3,2,1,0:T(8,128)(2,1)S(1)}, bf16[2,2,1,768,768]{4,3,2,1,0:T(8,128)(2,1)}, u32[]{:S(2)}) copy-start(bf16[2,2,1,768,768]{4,3,2,1,0:T(8,128)(2,1)} %tau_ref.1) | copy-start | bytes 14155780
  0.6 40.3 %copy-start.2 = (s32[2,4]{1,0:T(2,128)S(1)}, s32[2,4]{1,0:T(2,128)}, u32[]{:S(2)}) copy-start(s32[2,4]{1,0:T(2,128)} %perm_ref.3) | copy-start | bytes 100
  0.7 40.3 %copy-start.3 = (s32[2,4]{1,0:T(2,128)S(1)}, s32[2,4]{1,0:T(2,128)}, u32[]{:S(2)}) copy-start(s32[2,4]{1,0:T(2,128)} %sign_ref.3) | copy-start | bytes 100
  15.5 1.0 %copy-start = (bf16[384,384]{1,0:T(8,128)(2,1)S(1)}, bf16[384,384]{1,0:T(8,128)(2,1)}, u32[]{:S(2)}) copy-start(bf16[384,384]{1,0:T(8,128)(2,1)} %project.1) | copy-start | bytes 884740
  28.2 40.7 %collective-permute-start.1 = (bf16[384,384]{1,0:T(8,128)(2,1)S(1)}, bf16[384,384]{1,0:T(8,128)(2,1)S(1)}, u32[]{:S(2)}, u32[]{:S(2)}) collective-permute-start(bf16[384,384]{1,0:T(8,128)(2,1)S(1)} %bitcast.7), channel_id=1, source_target_pairs={{0,64},{1,72},{2,80},{3,88},{4,96},{5,104},{6,112},{7,120},{8,0},{... | collective-permute-start | bytes 884744 | tf_op jit(solution)/shard_map/ppermute | solution.py:279
  35.2 33.8 %collective-permute-start = (bf16[384,384]{1,0:T(8,128)(2,1)S(1)}, bf16[384,384]{1,0:T(8,128)(2,1)S(1)}, u32[]{:S(2)}, u32[]{:S(2)}) collective-permute-start(bf16[384,384]{1,0:T(8,128)(2,1)S(1)} %bitcast.8), channel_id=1, source_target_pairs={{0,0},{1,8},{2,16},{3,24},{4,32},{5,40},{6,48},{7,56},{8,64},{9,72... | collective-permute-start | bytes 884744 | tf_op jit(solution)/shard_map/ppermute | solution.py:279

commit v2 on v0

v2 whole, which is shorter than its diff:
```python
import functools
import math

import jax
import jax.numpy as jnp
from jax import lax
from jax.experimental import pallas as pl
from jax.experimental.pallas import tpu as pltpu
from jax.sharding import PartitionSpec as P

L = 32
NEV = 192
COLOR = 3
SPIN = 4
SITES = 32768
NDIM = SPIN * NEV
PAIR = 2 * NEV
LANE = 128
DEPTH = 4
MESH = pl.DeviceIdType.MESH
F32 = jnp.float32
BF16 = jnp.bfloat16
NT = (((1,), (1,)), ((), ()))
NN = (((1,), (0,)), ((), ()))


def dot(a, b, dims=NN):
    return lax.dot_general(a, b, dims, preferred_element_type=F32)


def load_phases(mom_ref, site_ref, phase):
    site = site_ref[...]
    first, second, third = site >> 10, (site >> 5) & (L - 1), site & (L - 1)
    for p in range(2):
        dotted = mom_ref[p, 0] * first + mom_ref[p, 1] * second + mom_ref[p, 2] * third
        angle = (dotted & (L - 1)).astype(F32) * (2.0 * math.pi / L)
        phase[2 * p] = jnp.cos(angle)
        phase[2 * p + 1] = jnp.sin(angle)


def project_chunk(vec, phase, cut, turned, acc, lanes):
    for j in range(lanes // LANE):
        span = slice(j * LANE, (j + 1) * LANE)
        real = vec[0, :, span].astype(F32)
        imag = vec[1, :, span].astype(F32)
        for p in range(2):
            cosine = phase[2 * p, cut, j : j + 1, :]
            sine = phase[2 * p + 1, cut, j : j + 1, :]
            turned[p * NEV : (p + 1) * NEV, span] = (cosine * real - sine * imag).astype(BF16)
            turned[PAIR + p * NEV : PAIR + (p + 1) * NEV, span] = (cosine * imag + sine * real).astype(BF16)
    plain = jnp.concatenate([vec[0], vec[1]], axis=0)
    acc[...] += dot(plain, turned[...], NT)


def arrange(pair, perm_ref, sign_ref, tau, spins, moved):
    for a in range(SPIN):
        cut = slice(a * NEV, (a + 1) * NEV)
        spins[pair, a, :, 0:NEV] = tau[0, pair, :, cut]
        spins[pair, a, :, NEV:PAIR] = tau[1, pair, :, cut]
    for q in range(2):
        for a in range(SPIN):
            into = perm_ref[q, a]
            sign = (2 * sign_ref[q, a] - 1) * jnp.where(into < SPIN // 2, 1, -1)
            block = spins[pair, into] * sign.astype(F32).astype(BF16)
            moved[pair, q, 0, :, a * NEV : (a + 1) * NEV] = block[:, 0:NEV]
            moved[pair, q, 1, :, a * NEV : (a + 1) * NEV] = block[:, NEV:PAIR]


def close_rows(pair, start, rows, table, spins, moved, mixed, out_ref):
    for a in range(SPIN):
        product = dot(spins[pair, a, pl.ds(start, rows), :], table[...]).astype(BF16)
        for c in range(2):
            for q in range(2):
                left = c * PAIR + q * NEV
                mixed[q, c, :, a * NEV : (a + 1) * NEV] = product[:, left : left + NEV]
    for q in range(2):
        real, imag = mixed[q, 0], mixed[q, 1]
        keep = pl.ds(start, rows)
        out_ref[q, 0, pair, keep, :] = (dot(real, moved[pair, q, 0], NT) + dot(imag, moved[pair, q, 1], NT)).astype(BF16)
        out_ref[q, 1, pair, keep, :] = (dot(imag, moved[pair, q, 0], NT) - dot(real, moved[pair, q, 1], NT)).astype(BF16)


def main_kernel(
    count, cuts, rows,
    mom_ref, perm_ref, sign_ref, site_ref, vec_hbm, tau_hbm,
    out_ref, sink_ref,
    phase, vecs, turned, acc, tau, spins, moved, mixed, part, held, whole, table,
    vec_sem, tau_sem, send_sem, recv_sem, back_send, back_recv, sink_send, sink_recv,
):
    time, me = lax.axis_index("ta"), lax.axis_index("gx")
    depth, lanes = vecs.shape[0], vecs.shape[-1]
    chunks = COLOR * cuts

    def fetch(i):
        span = pl.ds(pl.multiple_of(lax.rem(i, cuts) * lanes, lanes), lanes)
        return pltpu.make_async_copy(vec_hbm.at[:, i // cuts, :, span], vecs.at[lax.rem(i, depth)], vec_sem.at[lax.rem(i, depth)])

    for i in range(depth - 1):
        fetch(i).start()
    fetch_tau = pltpu.make_async_copy(tau_hbm, tau, tau_sem)
    fetch_tau.start()

    barrier = pltpu.get_barrier_semaphore()
    for hop in range(1, count):
        pl.semaphore_signal(barrier, inc=1, device_id={"gx": lax.rem(me + hop, count)}, device_id_type=MESH)
    for b in range(2):
        source = 2 * me + b
        holder = lax.rem(time + me - source - 1 + 4 * count, count)
        pl.semaphore_signal(barrier, inc=1, device_id={"ta": source, "gx": holder}, device_id_type=MESH)

    load_phases(mom_ref, site_ref, phase)
    acc[...] = jnp.zeros_like(acc)

    @pl.loop(0, chunks)
    def _(i):
        fetch(i).wait()

        @pl.when(i + depth - 1 < chunks)
        def _():
            fetch(i + depth - 1).start()

        project_chunk(vecs.at[lax.rem(i, depth)], phase, lax.rem(i, cuts), turned, acc, lanes)

    norm = 0.5 / math.sqrt(COLOR * SITES * NEV)
    half = count // 2
    width = PAIR // count
    real = (acc[0:NEV, 0:PAIR] + acc[NEV:PAIR, PAIR:NDIM]) * norm
    imag = (acc[0:NEV, PAIR:NDIM] - acc[NEV:PAIR, 0:PAIR]) * norm
    part[0:half] = real.astype(BF16).reshape(half, width, PAIR)
    part[half:count] = imag.astype(BF16).reshape(half, width, PAIR)

    pl.semaphore_wait(barrier, count + 1)
    copies = []
    for hop in range(1, count):
        peer = lax.rem(me + hop, count)
        copy = pltpu.make_async_remote_copy(
            src_ref=part.at[peer], dst_ref=held.at[hop],
            send_sem=send_sem.at[hop], recv_sem=recv_sem.at[hop],
            device_id={"gx": peer}, device_id_type=MESH,
        )
        copy.start()
        copies.append(copy)
    fetch_tau.wait()
    arrange(0, perm_ref, sign_ref, tau, spins, moved)
    total = part[me].astype(F32)
    for hop in range(1, count):
        copies[hop - 1].wait_recv()
        total = total + held[hop].astype(F32)
    whole[me] = total.astype(BF16)
    backs = []
    for hop in range(1, count):
        back = pltpu.make_async_remote_copy(
            src_ref=whole.at[me], dst_ref=whole.at[me],
            send_sem=back_send.at[hop], recv_sem=back_recv.at[hop],
            device_id={"gx": lax.rem(me + hop, count)}, device_id_type=MESH,
        )
        back.start()
        backs.append(back)
    arrange(1, perm_ref, sign_ref, tau, spins, moved)
    for hop in range(1, count):
        copies[hop - 1].wait_send()
        backs[hop - 1].wait()

    slot = lax.rem(time, 2)
    target = time // 2
    sinks = []
    for h in range(2):
        to = lax.rem(me - target + time + 1 + count, count) + h * count
        sink = pltpu.make_async_remote_copy(
            src_ref=whole, dst_ref=sink_ref.at[slot],
            send_sem=sink_send.at[h], recv_sem=sink_recv.at[slot],
            device_id={"ta": to, "gx": target}, device_id_type=MESH,
        )
        sink.start()
        sinks.append(sink)

    first = whole[0:half].reshape(NEV, PAIR)
    second = whole[half:count].reshape(NEV, PAIR)
    table[0:NEV, 0:PAIR] = first
    table[0:NEV, PAIR:NDIM] = second
    table[NEV:PAIR, 0:PAIR] = -second
    table[NEV:PAIR, PAIR:NDIM] = first

    blocks = NDIM // rows

    @pl.loop(0, 2 * blocks)
    def _(i):
        start = pl.multiple_of(lax.rem(i, blocks) * rows, rows)
        close_rows(i // blocks, start, rows, table, spins, moved, mixed, out_ref)

    for h in range(2):
        sinks[h].wait_send()
    for b in range(2):
        pltpu.make_async_remote_copy(
            src_ref=whole, dst_ref=sink_ref.at[b],
            send_sem=sink_send.at[b], recv_sem=sink_recv.at[b],
            device_id={"gx": lax.rem(me + 1, count)}, device_id_type=MESH,
        ).wait_recv()


def pinned(array):
    return pltpu.with_memory_space_constraint(array, pltpu.HBM)


def main_call(momenta, spin_perm, spin_sign, site_index, vectors, peram, count, chunk=1024, rows=384):
    sites = vectors.shape[-1]
    cuts = sites // chunk
    width = PAIR // count
    smem = pl.BlockSpec(memory_space=pltpu.SMEM)
    vmem = pl.BlockSpec(memory_space=pltpu.VMEM)
    hbm = pl.BlockSpec(memory_space=pltpu.HBM)
    dma = pltpu.SemaphoreType.DMA
    return pl.pallas_call(
        functools.partial(main_kernel, count, cuts, rows),
        out_shape=(
            pltpu.VMEM((2, 2, 2, NDIM, NDIM), BF16),
            pltpu.VMEM((2, count, width, PAIR), BF16),
        ),
        in_specs=[smem, smem, smem, vmem, hbm, hbm],
        out_specs=(vmem, vmem),
        scratch_shapes=[
            pltpu.VMEM((4, cuts, chunk // LANE, LANE), F32),
            pltpu.VMEM((DEPTH, 2, NEV, chunk), BF16),
            pltpu.VMEM((NDIM, chunk), BF16),
            pltpu.VMEM((PAIR, NDIM), F32),
            pltpu.VMEM((2, 2, NDIM, NDIM), BF16),
            pltpu.VMEM((2, SPIN, NDIM, PAIR), BF16),
            pltpu.VMEM((2, 2, 2, NDIM, NDIM), BF16),
            pltpu.VMEM((2, 2, rows, NDIM), BF16),
            pltpu.VMEM((count, width, PAIR), BF16),
            pltpu.VMEM((count, width, PAIR), BF16),
            pltpu.VMEM((count, width, PAIR), BF16),
            pltpu.VMEM((PAIR, NDIM), BF16),
            dma((DEPTH,)),
            dma,
            dma((count,)),
            dma((count,)),
            dma((count,)),
            dma((count,)),
            dma((2,)),
            dma((2,)),
        ],
        compiler_params=pltpu.CompilerParams(
            collective_id=0, has_side_effects=True, vmem_limit_bytes=42 * 1024 * 1024
        ),
        name="project_sum_close",
    )(momenta, spin_perm, spin_sign, site_index.reshape(cuts, chunk // LANE, LANE), pinned(vectors), pinned(peram))


def apply_kernel(perm_ref, sign_ref, elem_ref, x_ref, out0_ref, out1_ref, table):
    pair, r = pl.program_id(0), pl.program_id(1)

    @pl.when(r == 0)
    def _():
        for d in range(2):
            real = elem_ref[pair, 0:NEV, d * NEV : (d + 1) * NEV]
            imag = elem_ref[pair, NEV:PAIR, d * NEV : (d + 1) * NEV]
            table[d, 0:NEV, 0:NEV] = real
            table[d, 0:NEV, NEV:PAIR] = -imag
            table[d, NEV:PAIR, 0:NEV] = imag
            table[d, NEV:PAIR, NEV:PAIR] = real

    chiral = jnp.where(lax.broadcasted_iota(jnp.int32, (1, NDIM), 1) < NDIM // 2, 1.0, -1.0)
    weights = chiral * (0.5 / math.sqrt(NDIM))
    for d, out_ref in ((0, out0_ref), (1, out1_ref)):
        span = pl.ds(pl.multiple_of(perm_ref[d, r] * NEV, NEV), NEV)
        sign = (2 * sign_ref[d, r] - 1).astype(F32)
        stacked = jnp.concatenate([x_ref[1 - d, 0, pair, span, :], x_ref[1 - d, 1, pair, span, :]], axis=0)
        done = dot(table[d], stacked) * (weights * sign)
        out_ref[0, 0, 0] = done[0:NEV].astype(BF16)
        out_ref[1, 0, 0] = done[NEV:PAIR].astype(BF16)


def apply_sinks(elem, blocks, spin_perm, spin_sign, interpret=False):
    sinks = blocks.shape[2]
    shape = jax.ShapeDtypeStruct((2, sinks, 1, NDIM, NDIM), BF16)
    out_spec = pl.BlockSpec((2, 1, 1, NEV, NDIM), lambda i, j: (0, i, 0, j, 0))
    smem = pl.BlockSpec(memory_space=pltpu.SMEM)
    vmem = pl.BlockSpec(memory_space=pltpu.VMEM)
    return pl.pallas_call(
        apply_kernel,
        out_shape=(shape, shape),
        grid=(sinks, SPIN),
        in_specs=[smem, smem, vmem, vmem],
        out_specs=(out_spec, out_spec),
        scratch_shapes=[pltpu.VMEM((2, PAIR, PAIR), BF16)],
        compiler_params=pltpu.CompilerParams(
            dimension_semantics=("arbitrary", "arbitrary"), vmem_limit_bytes=24 * 1024 * 1024
        ),
        name="apply_sinks",
        interpret=interpret,
    )(spin_perm, spin_sign, elem, blocks)


def on_device(count, eigenvectors, site_index, momenta, perambulators, spin_perm, spin_sign):
    vectors = jnp.transpose(eigenvectors[0], (0, 2, 3, 1))
    blocks, elem = main_call(
        momenta, spin_perm, spin_sign, site_index, vectors, perambulators[:, :, 0], count
    )
    return apply_sinks(elem.reshape(2, PAIR, PAIR), blocks, spin_perm, spin_sign)


def solution(mesh):
    return jax.shard_map(
        functools.partial(on_device, mesh.shape["gx"]),
        mesh=mesh,
        in_specs=(
            P("ta", None, "gx", None, None),
            P("gx"),
            P(),
            P(None, "gx", "ta", None, None),
            P(),
            P(),
        ),
        out_specs=(P(None, "gx", "ta", None, None), P(None, "gx", "ta", None, None)),
        check_vma=False,
    )
```

time: 346 us -> 78.5 us (0.23)
  the two profiles are of different devices: /device:TPU:7 before, /device:TPU:96 now
where the time goes in v2:
time: 78.5 us; the launch traced here: 78.3 us
  Pallas kernels  74.9 us (95%)
  local copies, waits for them, and re-layouts  2.75 us (4%)
    pallas_call x1, Pallas kernels, main_call(): pl.pallas_call(functools.partial(main_kernel, count, cuts, rows), out_sha...  65.9 us
    pallas_call x1, Pallas kernels, apply_sinks(): pl.pallas_call(apply_kernel, out_shape=(shape, shape), grid=(sinks, SPIN)...  9 us
    unnamed x8, local copies, waits for them, and re-layouts  2.75 us

profile of v2, /device:TPU:96, one launch (start us, length us, event | category | flops | bytes accessed | tf_op | source)
XLA Modules:
  0.0 78.3 jit_solution(12672859484023889130)
XLA Ops:
  0.6 0.0 copy-start
  0.6 0.7 copy-done
  1.4 0.0 copy-start.1
  1.4 0.7 copy-done.1
  2.0 0.0 copy-start.2
  2.0 0.7 copy-done.2
  2.7 0.0 copy-start.3
  2.7 0.7 copy-done.3
  3.4 65.9 %project_sum_close.1 = (bf16[2,2,2,768,768]{4,3,2,1,0:T(8,128)(2,1)S(1)}, bf16[2,8,48,384]{3,2,1,0:T(8,128)(2,1)S(1)}) custom-call(s32[2,3]{1,0:T(2,128)S(1)} %copy-done.3, s32[2,4]{1,0:T(2,128)S(1)} %copy-done.1, s32[2,4]{1,0:T(2,128)S(1)} %copy-done.2, s32[4,8,128]{2,1,0:T(8,128)S(1)} %bitcast.7, bf16[2,3,192,4096]{3,2,1,0:T(8,128)(2,1)} %bitcast.8, ...), custom_call_target="tpu_custom_call" | custom-call | tf_op jit(solution)/shard_map/project_sum_close/pallas_call | solution.py:213
  69.3 9.0 %apply_sinks.1 = (bf16[2,2,1,768,768]{4,3,2,1,0:T(8,128)(2,1)}, bf16[2,2,1,768,768]{4,3,2,1,0:T(8,128)(2,1)}) custom-call(s32[2,4]{1,0:T(2,128)S(1)} %copy-done.1, s32[2,4]{1,0:T(2,128)S(1)} %copy-done.2, bf16[2,384,384]{2,1,0:T(8,128)(2,1)S(1)} %bitcast.6, bf16[2,2,2,768,768]{4,3,2,1,0:T(8,128)(2,1)S(1)} %get-tuple-element.5.x_ref), custom_call_target="tpu_custom_call" | custom-call | tf_op jit(solution)/shard_map/apply_sinks/pallas_call | solution.py:280
Async XLA Ops:
  0.6 0.7 copy-start
  1.4 0.7 copy-start.1
  2.0 0.7 copy-start.2
  2.7 0.7 copy-start.3

commit v3 on v2

--- a/solution.py
+++ b/solution.py
@@ -28,6 +28,20 @@
     return lax.dot_general(a, b, dims, preferred_element_type=F32)
 
 
+FIRST = (3, 5, 6, 0, 2, 4, 7, 1)
+TWIST = (0, 2, 6, 4, 5, 7, 3, 1)
+SOURCE = [[a ^ b for a in FIRST] for b in TWIST]
+TARGET = [[row.index(chip) for chip in range(8)] for row in SOURCE]
+
+
+def look_up(table, i, j):
+    found = 0
+    for a, row in enumerate(table):
+        for b, value in enumerate(row):
+            found = found + jnp.where((i == a) & (j == b), value, 0)
+    return found
+
+
 def load_phases(mom_ref, site_ref, phase):
     site = site_ref[...]
     first, second, third = site >> 10, (site >> 5) & (L - 1), site & (L - 1)
@@ -38,7 +52,7 @@
         phase[2 * p + 1] = jnp.sin(angle)
 
 
-def project_chunk(vec, phase, cut, turned, acc, lanes):
+def turn_chunk(vec, phase, cut, turned, lanes):
     for j in range(lanes // LANE):
         span = slice(j * LANE, (j + 1) * LANE)
         real = vec[0, :, span].astype(F32)
@@ -48,8 +62,6 @@
             sine = phase[2 * p + 1, cut, j : j + 1, :]
             turned[p * NEV : (p + 1) * NEV, span] = (cosine * real - sine * imag).astype(BF16)
             turned[PAIR + p * NEV : PAIR + (p + 1) * NEV, span] = (cosine * imag + sine * real).astype(BF16)
-    plain = jnp.concatenate([vec[0], vec[1]], axis=0)
-    acc[...] += dot(plain, turned[...], NT)
 
 
 def arrange(pair, perm_ref, sign_ref, tau, spins, moved):
@@ -82,44 +94,53 @@
 
 def main_kernel(
     count, cuts, rows,
-    mom_ref, perm_ref, sign_ref, site_ref, vec_hbm, tau_hbm,
+    mom_hbm, perm_hbm, sign_hbm, site_hbm, vec_hbm, tau_hbm,
     out_ref, sink_ref,
-    phase, vecs, turned, acc, tau, spins, moved, mixed, part, held, whole, table,
-    vec_sem, tau_sem, send_sem, recv_sem, back_send, back_recv, sink_send, sink_recv,
+    mom_ref, perm_ref, sign_ref, site_ref, phase, vecs, even, odd, acc, tau, spins, moved, mixed, part, held, whole, table,
+    small_sem, vec_sem, tau_sem, send_sem, recv_sem, back_send, back_recv, sink_send, sink_recv,
 ):
     time, me = lax.axis_index("ta"), lax.axis_index("gx")
     depth, lanes = vecs.shape[0], vecs.shape[-1]
     chunks = COLOR * cuts
+    small = ((mom_hbm, mom_ref), (site_hbm, site_ref), (perm_hbm, perm_ref), (sign_hbm, sign_ref))
+    small = [pltpu.make_async_copy(a, b, small_sem.at[k]) for k, (a, b) in enumerate(small)]
 
     def fetch(i):
-        span = pl.ds(pl.multiple_of(lax.rem(i, cuts) * lanes, lanes), lanes)
-        return pltpu.make_async_copy(vec_hbm.at[:, i // cuts, :, span], vecs.at[lax.rem(i, depth)], vec_sem.at[lax.rem(i, depth)])
-
-    for i in range(depth - 1):
+        source = vec_hbm.at[:, i // cuts, :, i % cuts * lanes : (i % cuts + 1) * lanes]
+        return pltpu.make_async_copy(source, vecs.at[i % depth], vec_sem.at[i % depth])
+
+    for copy in small:
+        copy.start()
+    for i in range(depth):
         fetch(i).start()
     fetch_tau = pltpu.make_async_copy(tau_hbm, tau, tau_sem)
     fetch_tau.start()
 
+    slot = lax.rem(time, 2)
+    sibling = {"ta": time + 1 - 2 * slot}
     barrier = pltpu.get_barrier_semaphore()
     for hop in range(1, count):
         pl.semaphore_signal(barrier, inc=1, device_id={"gx": lax.rem(me + hop, count)}, device_id_type=MESH)
-    for b in range(2):
-        source = 2 * me + b
-        holder = lax.rem(time + me - source - 1 + 4 * count, count)
-        pl.semaphore_signal(barrier, inc=1, device_id={"ta": source, "gx": holder}, device_id_type=MESH)
-
+    source = {"ta": 2 * me + slot, "gx": look_up(SOURCE, me, time // 2)}
+    pl.semaphore_signal(barrier, inc=1, device_id=source, device_id_type=MESH)
+    pl.semaphore_signal(barrier, inc=1, device_id=sibling, device_id_type=MESH)
+
+    small[0].wait()
+    small[1].wait()
     load_phases(mom_ref, site_ref, phase)
-    acc[...] = jnp.zeros_like(acc)
-
-    @pl.loop(0, chunks)
-    def _(i):
-        fetch(i).wait()
-
-        @pl.when(i + depth - 1 < chunks)
-        def _():
-            fetch(i + depth - 1).start()
-
-        project_chunk(vecs.at[lax.rem(i, depth)], phase, lax.rem(i, cuts), turned, acc, lanes)
+    fetch(0).wait()
+    turn_chunk(vecs.at[0], phase, 0, even, lanes)
+    for i in range(chunks):
+        if i + 1 < chunks:
+            fetch(i + 1).wait()
+            turn_chunk(vecs.at[(i + 1) % depth], phase, (i + 1) % cuts, even if i % 2 else odd, lanes)
+        plain = jnp.concatenate([vecs[i % depth, 0], vecs[i % depth, 1]], axis=0)
+        product = dot(plain, (odd if i % 2 else even)[...], NT)
+        acc[...] = product if i == 0 else acc[...] + product
+        if i + depth < chunks:
+            fetch(i + depth).start()
+    small[2].wait()
+    small[3].wait()
 
     norm = 0.5 / math.sqrt(COLOR * SITES * NEV)
     half = count // 2
@@ -161,18 +182,12 @@
         copies[hop - 1].wait_send()
         backs[hop - 1].wait()
 
-    slot = lax.rem(time, 2)
     target = time // 2
-    sinks = []
-    for h in range(2):
-        to = lax.rem(me - target + time + 1 + count, count) + h * count
-        sink = pltpu.make_async_remote_copy(
-            src_ref=whole, dst_ref=sink_ref.at[slot],
-            send_sem=sink_send.at[h], recv_sem=sink_recv.at[slot],
-            device_id={"ta": to, "gx": target}, device_id_type=MESH,
-        )
-        sink.start()
-        sinks.append(sink)
+    sink = pltpu.make_async_remote_copy(
+        src_ref=whole, dst_ref=sink_ref.at[slot], send_sem=sink_send.at[0], recv_sem=sink_recv.at[0],
+        device_id={"ta": 2 * look_up(TARGET, target, me) + slot, "gx": target}, device_id_type=MESH,
+    )
+    sink.start()
 
     first = whole[0:half].reshape(NEV, PAIR)
     second = whole[half:count].reshape(NEV, PAIR)
@@ -182,20 +197,24 @@
     table[NEV:PAIR, PAIR:NDIM] = first
 
     blocks = NDIM // rows
-
-    @pl.loop(0, 2 * blocks)
+    last = 2 * blocks - 1
+    onward = pltpu.make_async_remote_copy(
+        src_ref=sink_ref.at[slot], dst_ref=sink_ref.at[slot], send_sem=sink_send.at[1], recv_sem=sink_recv.at[1],
+        device_id=sibling, device_id_type=MESH,
+    )
+
+    @pl.loop(0, last + 1)
     def _(i):
+        @pl.when(i == last)
+        def _():
+            sink.wait_recv()
+            onward.start()
+
         start = pl.multiple_of(lax.rem(i, blocks) * rows, rows)
         close_rows(i // blocks, start, rows, table, spins, moved, mixed, out_ref)
 
-    for h in range(2):
-        sinks[h].wait_send()
-    for b in range(2):
-        pltpu.make_async_remote_copy(
-            src_ref=whole, dst_ref=sink_ref.at[b],
-            send_sem=sink_send.at[b], recv_sem=sink_recv.at[b],
-            device_id={"gx": lax.rem(me + 1, count)}, device_id_type=MESH,
-        ).wait_recv()
+    sink.wait_send()
+    onward.wait()
 
 
 def pinned(array):
@@ -206,7 +225,6 @@
     sites = vectors.shape[-1]
     cuts = sites // chunk
     width = PAIR // count
-    smem = pl.BlockSpec(memory_space=pltpu.SMEM)
     vmem = pl.BlockSpec(memory_space=pltpu.VMEM)
     hbm = pl.BlockSpec(memory_space=pltpu.HBM)
     dma = pltpu.SemaphoreType.DMA
@@ -216,11 +234,16 @@
             pltpu.VMEM((2, 2, 2, NDIM, NDIM), BF16),
             pltpu.VMEM((2, count, width, PAIR), BF16),
         ),
-        in_specs=[smem, smem, smem, vmem, hbm, hbm],
+        in_specs=[hbm] * 6,
         out_specs=(vmem, vmem),
         scratch_shapes=[
+            pltpu.SMEM(momenta.shape, jnp.int32),
+            pltpu.SMEM(spin_perm.shape, jnp.int32),
+            pltpu.SMEM(spin_sign.shape, jnp.int32),
+            pltpu.VMEM((cuts, chunk // LANE, LANE), jnp.int32),
             pltpu.VMEM((4, cuts, chunk // LANE, LANE), F32),
             pltpu.VMEM((DEPTH, 2, NEV, chunk), BF16),
+            pltpu.VMEM((NDIM, chunk), BF16),
             pltpu.VMEM((NDIM, chunk), BF16),
             pltpu.VMEM((PAIR, NDIM), F32),
             pltpu.VMEM((2, 2, NDIM, NDIM), BF16),
@@ -231,6 +254,7 @@
             pltpu.VMEM((count, width, PAIR), BF16),
             pltpu.VMEM((count, width, PAIR), BF16),
             pltpu.VMEM((PAIR, NDIM), BF16),
+            dma((4,)),
             dma((DEPTH,)),
             dma,
             dma((count,)),
@@ -244,7 +268,7 @@
             collective_id=0, has_side_effects=True, vmem_limit_bytes=42 * 1024 * 1024
         ),
         name="project_sum_close",
-    )(momenta, spin_perm, spin_sign, site_index.reshape(cuts, chunk // LANE, LANE), pinned(vectors), pinned(peram))
+    )(*map(pinned, (momenta, spin_perm, spin_sign, site_index.reshape(cuts, chunk // LANE, LANE), vectors, peram)))
 
 
 def apply_kernel(perm_ref, sign_ref, elem_ref, x_ref, out0_ref, out1_ref, table):

time: 78.5 us -> 67.5 us (0.86)
  the two profiles are of different devices: /device:TPU:96 before, /device:TPU:7 now
where the time goes in v3:
time: 67.5 us; the launch traced here: 67.4 us
  Pallas kernels  66.7 us (99%)
    pallas_call x1, Pallas kernels, main_call(): pl.pallas_call(functools.partial(main_kernel, count, cuts, rows), out_sha...  57.8 us
    pallas_call x1, Pallas kernels, apply_sinks(): pl.pallas_call(apply_kernel, out_shape=(shape, shape), grid=(sinks, SPIN)...  8.96 us

profile of v3, /device:TPU:7, one launch (start us, length us, event | category | flops | bytes accessed | tf_op | source)
XLA Modules:
  0.0 67.4 jit_solution(679250242986419519)
XLA Ops:
  0.6 0.0 copy-start
  0.6 0.0 copy-start.1
  0.7 57.8 %project_sum_close.1 = (bf16[2,2,2,768,768]{4,3,2,1,0:T(8,128)(2,1)S(1)}, bf16[2,8,48,384]{3,2,1,0:T(8,128)(2,1)S(1)}) custom-call(s32[2,3]{1,0:T(2,128)} %mom_hbm.1, s32[2,4]{1,0:T(2,128)} %perm_ref.1, s32[2,4]{1,0:T(2,128)} %sign_ref.1, s32[4,8,128]{2,1,0:T(8,128)} %bitcast.9, bf16[2,3,192,4096]{3,2,1,0:T(8,128)(2,1)} %bitcast.7, ...), custom_call_target="tpu_custom_call" | custom-call | tf_op jit(solution)/shard_map/project_sum_close/pallas_call | solution.py:231
  58.4 0.0 copy-done
  58.4 0.0 copy-done.1
  58.4 9.0 %apply_sinks.1 = (bf16[2,2,1,768,768]{4,3,2,1,0:T(8,128)(2,1)}, bf16[2,2,1,768,768]{4,3,2,1,0:T(8,128)(2,1)}) custom-call(s32[2,4]{1,0:T(2,128)S(1)} %copy-done, s32[2,4]{1,0:T(2,128)S(1)} %copy-done.1, bf16[2,384,384]{2,1,0:T(8,128)(2,1)S(1)} %bitcast.6, bf16[2,2,2,768,768]{4,3,2,1,0:T(8,128)(2,1)S(1)} %get-tuple-element.5.x_ref), custom_call_target="tpu_custom_call" | custom-call | tf_op jit(solution)/shard_map/apply_sinks/pallas_call | solution.py:304
Async XLA Ops:
  0.6 57.8 %copy-start = (s32[2,4]{1,0:T(2,128)S(1)}, s32[2,4]{1,0:T(2,128)}, u32[]{:S(2)}) copy-start(s32[2,4]{1,0:T(2,128)} %perm_ref.1) | copy-start | bytes 100
  0.6 57.8 %copy-start.1 = (s32[2,4]{1,0:T(2,128)S(1)}, s32[2,4]{1,0:T(2,128)}, u32[]{:S(2)}) copy-start(s32[2,4]{1,0:T(2,128)} %sign_ref.1) | copy-start | bytes 100

commit v4 on v3

--- a/solution.py
+++ b/solution.py
@@ -16,7 +16,7 @@
 NDIM = SPIN * NEV
 PAIR = 2 * NEV
 LANE = 128
-DEPTH = 4
+DEPTH = 3
 MESH = pl.DeviceIdType.MESH
 F32 = jnp.float32
 BF16 = jnp.bfloat16
@@ -48,55 +48,68 @@
     for p in range(2):
         dotted = mom_ref[p, 0] * first + mom_ref[p, 1] * second + mom_ref[p, 2] * third
         angle = (dotted & (L - 1)).astype(F32) * (2.0 * math.pi / L)
-        phase[2 * p] = jnp.cos(angle)
-        phase[2 * p + 1] = jnp.sin(angle)
+        for k, value in enumerate((jnp.cos(angle), jnp.sin(angle))):
+            phase[2 * p + k] = jnp.broadcast_to(value[:, :, None, :], value.shape[:2] + (8, LANE))
 
 
 def turn_chunk(vec, phase, cut, turned, lanes):
     for j in range(lanes // LANE):
         span = slice(j * LANE, (j + 1) * LANE)
-        real = vec[0, :, span].astype(F32)
-        imag = vec[1, :, span].astype(F32)
+        real = vec[0, :, span].astype(F32).reshape(NEV // 8, 8, LANE)
+        imag = vec[1, :, span].astype(F32).reshape(NEV // 8, 8, LANE)
         for p in range(2):
-            cosine = phase[2 * p, cut, j : j + 1, :]
-            sine = phase[2 * p + 1, cut, j : j + 1, :]
-            turned[p * NEV : (p + 1) * NEV, span] = (cosine * real - sine * imag).astype(BF16)
-            turned[PAIR + p * NEV : PAIR + (p + 1) * NEV, span] = (cosine * imag + sine * real).astype(BF16)
-
-
-def arrange(pair, perm_ref, sign_ref, tau, spins, moved):
+            cosine = phase[2 * p, cut, j][None]
+            sine = phase[2 * p + 1, cut, j][None]
+            first = (cosine * real - sine * imag).reshape(NEV, LANE)
+            second = (cosine * imag + sine * real).reshape(NEV, LANE)
+            turned[p * NEV : (p + 1) * NEV, span] = first.astype(BF16)
+            turned[PAIR + p * NEV : PAIR + (p + 1) * NEV, span] = second.astype(BF16)
+
+
+def arrange(pair, perm_ref, sign_ref, tau, spins, moved, rows=128):
+    @pl.loop(0, NDIM // rows)
+    def _(i):
+        keep = pl.ds(pl.multiple_of(i * rows, rows), rows)
+        for a in range(SPIN):
+            cut = slice(a * NEV, (a + 1) * NEV)
+            spins[pair, a, keep, 0:NEV] = tau[0, pair, keep, cut]
+            spins[pair, a, keep, NEV:PAIR] = tau[1, pair, keep, cut]
+        for q in range(2):
+            for a in range(SPIN):
+                into = perm_ref[q, a]
+                sign = (2 * sign_ref[q, a] - 1) * jnp.where(into < SPIN // 2, 1, -1)
+                block = spins[pair, into, keep, :] * sign.astype(F32).astype(BF16)
+                moved[pair, q, 0, keep, a * NEV : (a + 1) * NEV] = block[:, 0:NEV]
+                moved[pair, q, 1, keep, a * NEV : (a + 1) * NEV] = block[:, NEV:PAIR]
+            real, imag = moved[pair, q, 0, keep, :], moved[pair, q, 1, keep, :]
+            moved[pair, q, 2, keep, :] = (real.astype(F32) - imag.astype(F32)).astype(BF16)
+
+
+def close_rows(pair, start, rows, table, spins, moved, mixed, out_ref, before):
     for a in range(SPIN):
-        cut = slice(a * NEV, (a + 1) * NEV)
-        spins[pair, a, :, 0:NEV] = tau[0, pair, :, cut]
-        spins[pair, a, :, NEV:PAIR] = tau[1, pair, :, cut]
-    for q in range(2):
-        for a in range(SPIN):
-            into = perm_ref[q, a]
-            sign = (2 * sign_ref[q, a] - 1) * jnp.where(into < SPIN // 2, 1, -1)
-            block = spins[pair, into] * sign.astype(F32).astype(BF16)
-            moved[pair, q, 0, :, a * NEV : (a + 1) * NEV] = block[:, 0:NEV]
-            moved[pair, q, 1, :, a * NEV : (a + 1) * NEV] = block[:, NEV:PAIR]
-
-
-def close_rows(pair, start, rows, table, spins, moved, mixed, out_ref):
-    for a in range(SPIN):
-        product = dot(spins[pair, a, pl.ds(start, rows), :], table[...]).astype(BF16)
-        for c in range(2):
+        product = dot(spins[pair, a, pl.ds(start, rows), :], table[...])
+        real, imag = product[:, 0:PAIR], product[:, PAIR:NDIM]
+        for c, value in enumerate((real, imag, real + imag)):
+            value = value.astype(BF16)
             for q in range(2):
-                left = c * PAIR + q * NEV
-                mixed[q, c, :, a * NEV : (a + 1) * NEV] = product[:, left : left + NEV]
-    for q in range(2):
-        real, imag = mixed[q, 0], mixed[q, 1]
-        keep = pl.ds(start, rows)
-        out_ref[q, 0, pair, keep, :] = (dot(real, moved[pair, q, 0], NT) + dot(imag, moved[pair, q, 1], NT)).astype(BF16)
-        out_ref[q, 1, pair, keep, :] = (dot(imag, moved[pair, q, 0], NT) - dot(real, moved[pair, q, 1], NT)).astype(BF16)
+                mixed[q, c, :, a * NEV : (a + 1) * NEV] = value[:, q * NEV : (q + 1) * NEV]
+    keep = pl.ds(start, rows)
+
+    @pl.loop(0, 2)
+    def _(q):
+        before(q)
+        first = dot(mixed[q, 0], moved[pair, q, 0], NT)
+        second = dot(mixed[q, 1], moved[pair, q, 1], NT)
+        third = dot(mixed[q, 2], moved[pair, q, 2], NT)
+        out_ref[q, 0, pair, keep, :] = (first + second).astype(BF16)
+        out_ref[q, 1, pair, keep, :] = (third - first + second).astype(BF16)
 
 
 def main_kernel(
     count, cuts, rows,
     mom_hbm, perm_hbm, sign_hbm, site_hbm, vec_hbm, tau_hbm,
     out_ref, sink_ref,
-    mom_ref, perm_ref, sign_ref, site_ref, phase, vecs, even, odd, acc, tau, spins, moved, mixed, part, held, whole, table,
+    mom_ref, perm_ref, sign_ref, site_ref, phase, vecs, turned, acc, tau, spins, moved, mixed, part, held, whole, table,
     small_sem, vec_sem, tau_sem, send_sem, recv_sem, back_send, back_recv, sink_send, sink_recv,
 ):
     time, me = lax.axis_index("ta"), lax.axis_index("gx")
@@ -106,8 +119,9 @@
     small = [pltpu.make_async_copy(a, b, small_sem.at[k]) for k, (a, b) in enumerate(small)]
 
     def fetch(i):
-        source = vec_hbm.at[:, i // cuts, :, i % cuts * lanes : (i % cuts + 1) * lanes]
-        return pltpu.make_async_copy(source, vecs.at[i % depth], vec_sem.at[i % depth])
+        span = pl.ds(pl.multiple_of(lax.rem(i, cuts) * lanes, lanes), lanes)
+        turn = lax.rem(i, depth)
+        return pltpu.make_async_copy(vec_hbm.at[:, i // cuts, :, span], vecs.at[turn], vec_sem.at[turn])
 
     for copy in small:
         copy.start()
@@ -129,16 +143,23 @@
     small[1].wait()
     load_phases(mom_ref, site_ref, phase)
     fetch(0).wait()
-    turn_chunk(vecs.at[0], phase, 0, even, lanes)
-    for i in range(chunks):
-        if i + 1 < chunks:
-            fetch(i + 1).wait()
-            turn_chunk(vecs.at[(i + 1) % depth], phase, (i + 1) % cuts, even if i % 2 else odd, lanes)
-        plain = jnp.concatenate([vecs[i % depth, 0], vecs[i % depth, 1]], axis=0)
-        product = dot(plain, (odd if i % 2 else even)[...], NT)
-        acc[...] = product if i == 0 else acc[...] + product
-        if i + depth < chunks:
+    acc[...] = jnp.zeros_like(acc)
+
+    @pl.loop(0, chunks)
+    def _(i):
+        @pl.when(i > 0)
+        def _():
+            fetch(i).wait()
+
+        own = vecs.at[lax.rem(i, depth)]
+        turn_chunk(own, phase, lax.rem(i, cuts), turned, lanes)
+        plain = jnp.concatenate([own[0], own[1]], axis=0)
+        acc[...] += dot(plain, turned[...], NT)
+
+        @pl.when(i + depth < chunks)
+        def _():
             fetch(i + depth).start()
+
     small[2].wait()
     small[3].wait()
 
@@ -205,13 +226,14 @@
 
     @pl.loop(0, last + 1)
     def _(i):
-        @pl.when(i == last)
-        def _():
-            sink.wait_recv()
-            onward.start()
+        def before(q):
+            @pl.when((i == last) & (q == 1))
+            def _():
+                sink.wait_recv()
+                onward.start()
 
         start = pl.multiple_of(lax.rem(i, blocks) * rows, rows)
-        close_rows(i // blocks, start, rows, table, spins, moved, mixed, out_ref)
+        close_rows(i // blocks, start, rows, table, spins, moved, mixed, out_ref, before)
 
     sink.wait_send()
     onward.wait()
@@ -221,7 +243,7 @@
     return pltpu.with_memory_space_constraint(array, pltpu.HBM)
 
 
-def main_call(momenta, spin_perm, spin_sign, site_index, vectors, peram, count, chunk=1024, rows=384):
+def main_call(momenta, spin_perm, spin_sign, site_index, vectors, peram, count, chunk=2048, rows=384):
     sites = vectors.shape[-1]
     cuts = sites // chunk
     width = PAIR // count
@@ -241,15 +263,14 @@
             pltpu.SMEM(spin_perm.shape, jnp.int32),
             pltpu.SMEM(spin_sign.shape, jnp.int32),
             pltpu.VMEM((cuts, chunk // LANE, LANE), jnp.int32),
-            pltpu.VMEM((4, cuts, chunk // LANE, LANE), F32),
+            pltpu.VMEM((4, cuts, chunk // LANE, 8, LANE), F32),
             pltpu.VMEM((DEPTH, 2, NEV, chunk), BF16),
-            pltpu.VMEM((NDIM, chunk), BF16),
             pltpu.VMEM((NDIM, chunk), BF16),
             pltpu.VMEM((PAIR, NDIM), F32),
             pltpu.VMEM((2, 2, NDIM, NDIM), BF16),
             pltpu.VMEM((2, SPIN, NDIM, PAIR), BF16),
-            pltpu.VMEM((2, 2, 2, NDIM, NDIM), BF16),
-            pltpu.VMEM((2, 2, rows, NDIM), BF16),
+            pltpu.VMEM((2, 2, 3, NDIM, NDIM), BF16),
+            pltpu.VMEM((2, 3, rows, NDIM), BF16),
             pltpu.VMEM((count, width, PAIR), BF16),
             pltpu.VMEM((count, width, PAIR), BF16),
             pltpu.VMEM((count, width, PAIR), BF16),
@@ -265,55 +286,101 @@
             dma((2,)),
         ],
         compiler_params=pltpu.CompilerParams(
-            collective_id=0, has_side_effects=True, vmem_limit_bytes=42 * 1024 * 1024
+            collective_id=0, has_side_effects=True, vmem_limit_bytes=48 * 1024 * 1024
         ),
         name="project_sum_close",
     )(*map(pinned, (momenta, spin_perm, spin_sign, site_index.reshape(cuts, chunk // LANE, LANE), vectors, peram)))
 
 
-def apply_kernel(perm_ref, sign_ref, elem_ref, x_ref, out0_ref, out1_ref, table):
-    pair, r = pl.program_id(0), pl.program_id(1)
-
-    @pl.when(r == 0)
-    def _():
-        for d in range(2):
-            real = elem_ref[pair, 0:NEV, d * NEV : (d + 1) * NEV]
-            imag = elem_ref[pair, NEV:PAIR, d * NEV : (d + 1) * NEV]
-            table[d, 0:NEV, 0:NEV] = real
-            table[d, 0:NEV, NEV:PAIR] = -imag
-            table[d, NEV:PAIR, 0:NEV] = imag
-            table[d, NEV:PAIR, NEV:PAIR] = real
-
+def apply_kernel(group, perm_hbm, sign_hbm, elem_ref, x_ref, out0_hbm, out1_hbm, perm_ref, sign_ref, table, stage, small_sem, out_sem):
+    sinks = x_ref.shape[2]
+    parts = SPIN // group
+    small = [
+        pltpu.make_async_copy(perm_hbm, perm_ref, small_sem.at[0]),
+        pltpu.make_async_copy(sign_hbm, sign_ref, small_sem.at[1]),
+    ]
+    for copy in small:
+        copy.start()
+
+    @pl.loop(0, 2 * sinks)
+    def _(n):
+        pair, d = n // 2, lax.rem(n, 2)
+        both_real, both_imag = elem_ref[pair, 0:NEV], elem_ref[pair, NEV:PAIR]
+        real = jnp.where(d == 0, both_real[:, 0:NEV], both_real[:, NEV:PAIR])
+        imag = jnp.where(d == 0, both_imag[:, 0:NEV], both_imag[:, NEV:PAIR])
+        table[n, 0:NEV, 0:NEV] = real
+        table[n, 0:NEV, NEV:PAIR] = -imag
+        table[n, NEV:PAIR, 0:NEV] = imag
+        table[n, NEV:PAIR, NEV:PAIR] = real
+
+    for copy in small:
+        copy.wait()
     chiral = jnp.where(lax.broadcasted_iota(jnp.int32, (1, NDIM), 1) < NDIM // 2, 1.0, -1.0)
     weights = chiral * (0.5 / math.sqrt(NDIM))
-    for d, out_ref in ((0, out0_ref), (1, out1_ref)):
-        span = pl.ds(pl.multiple_of(perm_ref[d, r] * NEV, NEV), NEV)
-        sign = (2 * sign_ref[d, r] - 1).astype(F32)
-        stacked = jnp.concatenate([x_ref[1 - d, 0, pair, span, :], x_ref[1 - d, 1, pair, span, :]], axis=0)
-        done = dot(table[d], stacked) * (weights * sign)
-        out_ref[0, 0, 0] = done[0:NEV].astype(BF16)
-        out_ref[1, 0, 0] = done[NEV:PAIR].astype(BF16)
-
-
-def apply_sinks(elem, blocks, spin_perm, spin_sign, interpret=False):
+    steps = sinks * 2 * parts
+
+    def where(i):
+        n, part = i // parts, lax.rem(i, parts)
+        return n, n // 2, lax.rem(n, 2), part, lax.rem(i, 2)
+
+    def store(i, out_hbm):
+        n, pair, d, part, slot = where(i)
+        keep = pl.ds(pl.multiple_of(part * group * NEV, group * NEV), group * NEV)
+        return pltpu.make_async_copy(stage.at[slot], out_hbm.at[:, pair, 0, keep, :], out_sem.at[slot])
+
+    @pl.loop(0, steps)
+    def _(i):
+        n, pair, d, part, slot = where(i)
+
+        @pl.when(i >= 2)
+        def _():
+            store(i, out0_hbm).wait()
+
+        wide = []
+        for r in range(group):
+            span = pl.ds(pl.multiple_of(perm_ref[d, part * group + r] * NEV, NEV), NEV)
+            wide.append(jnp.concatenate([x_ref[1 - d, 0, pair, span, :], x_ref[1 - d, 1, pair, span, :]], axis=0))
+        done = dot(table[n], jnp.concatenate(wide, axis=1))
+        for r in range(group):
+            sign = (2 * sign_ref[d, part * group + r] - 1).astype(F32)
+            block = done[:, r * NDIM : (r + 1) * NDIM] * (weights * sign)
+            stage[slot, 0, r * NEV : (r + 1) * NEV] = block[0:NEV].astype(BF16)
+            stage[slot, 1, r * NEV : (r + 1) * NEV] = block[NEV:PAIR].astype(BF16)
+
+        @pl.when(d == 0)
+        def _():
+            store(i, out0_hbm).start()
+
+        @pl.when(d == 1)
+        def _():
+            store(i, out1_hbm).start()
+
+    for i in (steps - 2, steps - 1):
+        store(i, out0_hbm).wait()
+
+
+def apply_sinks(elem, blocks, spin_perm, spin_sign, group=4, interpret=False):
     sinks = blocks.shape[2]
     shape = jax.ShapeDtypeStruct((2, sinks, 1, NDIM, NDIM), BF16)
-    out_spec = pl.BlockSpec((2, 1, 1, NEV, NDIM), lambda i, j: (0, i, 0, j, 0))
-    smem = pl.BlockSpec(memory_space=pltpu.SMEM)
     vmem = pl.BlockSpec(memory_space=pltpu.VMEM)
+    hbm = pl.BlockSpec(memory_space=pltpu.HBM)
     return pl.pallas_call(
-        apply_kernel,
+        functools.partial(apply_kernel, group),
         out_shape=(shape, shape),
-        grid=(sinks, SPIN),
-        in_specs=[smem, smem, vmem, vmem],
-        out_specs=(out_spec, out_spec),
-        scratch_shapes=[pltpu.VMEM((2, PAIR, PAIR), BF16)],
-        compiler_params=pltpu.CompilerParams(
-            dimension_semantics=("arbitrary", "arbitrary"), vmem_limit_bytes=24 * 1024 * 1024
-        ),
+        in_specs=[hbm, hbm, vmem, vmem],
+        out_specs=(hbm, hbm),
+        scratch_shapes=[
+            pltpu.SMEM(spin_perm.shape, jnp.int32),
+            pltpu.SMEM(spin_sign.shape, jnp.int32),
+            pltpu.VMEM((2 * sinks, PAIR, PAIR), BF16),
+            pltpu.VMEM((2, 2, group * NEV, NDIM), BF16),
+            pltpu.SemaphoreType.DMA((2,)),
+            pltpu.SemaphoreType.DMA((2,)),
+        ],
+        compiler_params=pltpu.CompilerParams(vmem_limit_bytes=24 * 1024 * 1024),
         name="apply_sinks",
         interpret=interpret,
-    )(spin_perm, spin_sign, elem, blocks)
+    )(pinned(spin_perm), pinned(spin_sign), elem, blocks)
 
 
 def on_device(count, eigenvectors, site_index, momenta, perambulators, spin_perm, spin_sign):

time: 67.5 us -> 54.9 us (0.81)
  Pallas kernels: 66.7 us -> 53.9 us
    pallas_call x1, Pallas kernels: 57.8 us -> 45.8 us  [main_call(): pl.pallas_call(functools.partial(main_kernel, count, cuts, rows), out_sha...]
    pallas_call x1, Pallas kernels: 8.96 us -> 8.13 us  [apply_sinks(): pl.pallas_call(functools.partial(apply_kernel, group), out_shape=(shape,...]
where the time goes in v4:
time: 54.9 us; the launch traced here: 54.5 us
  Pallas kernels  53.9 us (98%)
  between operations  0.64 us (1%)
    pallas_call x1, Pallas kernels, main_call(): pl.pallas_call(functools.partial(main_kernel, count, cuts, rows), out_sha...  45.8 us
    pallas_call x1, Pallas kernels, apply_sinks(): pl.pallas_call(functools.partial(apply_kernel, group), out_shape=(shape,...  8.13 us

profile of v4, /device:TPU:7, one launch (start us, length us, event | category | flops | bytes accessed | tf_op | source)
XLA Modules:
  0.0 54.5 jit_solution(10504025417389564895)
XLA Ops:
  0.6 45.8 %project_sum_close.1 = (bf16[2,2,2,768,768]{4,3,2,1,0:T(8,128)(2,1)S(1)}, bf16[2,8,48,384]{3,2,1,0:T(8,128)(2,1)S(1)}) custom-call(s32[2,3]{1,0:T(2,128)} %mom_hbm.1, s32[2,4]{1,0:T(2,128)} %perm_hbm.3, s32[2,4]{1,0:T(2,128)} %sign_hbm.3, s32[2,16,128]{2,1,0:T(8,128)} %bitcast.9, bf16[2,3,192,4096]{3,2,1,0:T(8,128)(2,1)} %bitcast.7, ...), custom_call_target="tpu_custom_call" | custom-call | tf_op jit(solution)/shard_map/project_sum_close/pallas_call | solution.py:253
  46.4 8.1 %apply_sinks.1 = (bf16[2,2,1,768,768]{4,3,2,1,0:T(8,128)(2,1)}, bf16[2,2,1,768,768]{4,3,2,1,0:T(8,128)(2,1)}) custom-call(s32[2,4]{1,0:T(2,128)} %perm_hbm.3, s32[2,4]{1,0:T(2,128)} %sign_hbm.3, bf16[2,384,384]{2,1,0:T(8,128)(2,1)S(1)} %bitcast.6, bf16[2,2,2,768,768]{4,3,2,1,0:T(8,128)(2,1)S(1)} %get-tuple-element.5.x_ref), custom_call_target="tpu_custom_call" | custom-call | tf_op jit(solution)/shard_map/apply_sinks/pallas_call | solution.py:367

commit v5 on v4

--- a/solution.py
+++ b/solution.py
@@ -16,6 +16,7 @@
 NDIM = SPIN * NEV
 PAIR = 2 * NEV
 LANE = 128
+WIDTH = 256
 DEPTH = 3
 MESH = pl.DeviceIdType.MESH
 F32 = jnp.float32
@@ -98,11 +99,15 @@
     @pl.loop(0, 2)
     def _(q):
         before(q)
-        first = dot(mixed[q, 0], moved[pair, q, 0], NT)
-        second = dot(mixed[q, 1], moved[pair, q, 1], NT)
-        third = dot(mixed[q, 2], moved[pair, q, 2], NT)
-        out_ref[q, 0, pair, keep, :] = (first + second).astype(BF16)
-        out_ref[q, 1, pair, keep, :] = (third - first + second).astype(BF16)
+        for left in range(0, NDIM, WIDTH):
+            cols = slice(left, left + WIDTH)
+            first = dot(mixed[q, 0], moved[pair, q, 0, cols], NT)
+            second = dot(mixed[q, 1], moved[pair, q, 1, cols], NT)
+            third = dot(mixed[q, 2], moved[pair, q, 2, cols], NT)
+            out_ref[q, 0, pair, keep, cols] = (first + second).astype(BF16)
+            imag = third - first + second
+            out_ref[q, 1, pair, keep, cols] = imag.astype(BF16)
+            out_ref[q, 2, pair, keep, cols] = (first + second + imag).astype(BF16)
 
 
 def main_kernel(
@@ -253,7 +258,7 @@
     return pl.pallas_call(
         functools.partial(main_kernel, count, cuts, rows),
         out_shape=(
-            pltpu.VMEM((2, 2, 2, NDIM, NDIM), BF16),
+            pltpu.VMEM((2, 3, 2, NDIM, NDIM), BF16),
             pltpu.VMEM((2, count, width, PAIR), BF16),
         ),
         in_specs=[hbm] * 6,
@@ -286,7 +291,7 @@
             dma((2,)),
         ],
         compiler_params=pltpu.CompilerParams(
-            collective_id=0, has_side_effects=True, vmem_limit_bytes=48 * 1024 * 1024
+            collective_id=0, has_side_effects=True, vmem_limit_bytes=45 * 1024 * 1024
         ),
         name="project_sum_close",
     )(*map(pinned, (momenta, spin_perm, spin_sign, site_index.reshape(cuts, chunk // LANE, LANE), vectors, peram)))
@@ -308,10 +313,9 @@
         both_real, both_imag = elem_ref[pair, 0:NEV], elem_ref[pair, NEV:PAIR]
         real = jnp.where(d == 0, both_real[:, 0:NEV], both_real[:, NEV:PAIR])
         imag = jnp.where(d == 0, both_imag[:, 0:NEV], both_imag[:, NEV:PAIR])
-        table[n, 0:NEV, 0:NEV] = real
-        table[n, 0:NEV, NEV:PAIR] = -imag
-        table[n, NEV:PAIR, 0:NEV] = imag
-        table[n, NEV:PAIR, NEV:PAIR] = real
+        table[n, 0] = real
+        table[n, 1] = imag
+        table[n, 2] = (real.astype(F32) + imag.astype(F32)).astype(BF16)
 
     for copy in small:
         copy.wait()
@@ -336,16 +340,17 @@
         def _():
             store(i, out0_hbm).wait()
 
-        wide = []
         for r in range(group):
             span = pl.ds(pl.multiple_of(perm_ref[d, part * group + r] * NEV, NEV), NEV)
-            wide.append(jnp.concatenate([x_ref[1 - d, 0, pair, span, :], x_ref[1 - d, 1, pair, span, :]], axis=0))
-        done = dot(table[n], jnp.concatenate(wide, axis=1))
-        for r in range(group):
-            sign = (2 * sign_ref[d, part * group + r] - 1).astype(F32)
-            block = done[:, r * NDIM : (r + 1) * NDIM] * (weights * sign)
-            stage[slot, 0, r * NEV : (r + 1) * NEV] = block[0:NEV].astype(BF16)
-            stage[slot, 1, r * NEV : (r + 1) * NEV] = block[NEV:PAIR].astype(BF16)
+            signed = weights * (2 * sign_ref[d, part * group + r] - 1).astype(F32)
+            rows = slice(r * NEV, (r + 1) * NEV)
+            for left in range(0, NDIM, WIDTH):
+                cols = slice(left, left + WIDTH)
+                first = dot(table[n, 0], x_ref[1 - d, 0, pair, span, cols])
+                second = dot(table[n, 1], x_ref[1 - d, 1, pair, span, cols])
+                third = dot(table[n, 2], x_ref[1 - d, 2, pair, span, cols])
+                stage[slot, 0, rows, cols] = ((first - second) * signed[:, cols]).astype(BF16)
+                stage[slot, 1, rows, cols] = ((third - first - second) * signed[:, cols]).astype(BF16)
 
         @pl.when(d == 0)
         def _():
@@ -372,7 +377,7 @@
         scratch_shapes=[
             pltpu.SMEM(spin_perm.shape, jnp.int32),
             pltpu.SMEM(spin_sign.shape, jnp.int32),
-            pltpu.VMEM((2 * sinks, PAIR, PAIR), BF16),
+            pltpu.VMEM((2 * sinks, 3, NEV, NEV), BF16),
             pltpu.VMEM((2, 2, group * NEV, NDIM), BF16),
             pltpu.SemaphoreType.DMA((2,)),
             pltpu.SemaphoreType.DMA((2,)),

time: 54.9 us -> 53.7 us (0.978)
  Pallas kernels: 53.9 us -> 52.6 us
    pallas_call x1, Pallas kernels: 8.13 us -> 6.87 us  [apply_sinks(): pl.pallas_call(functools.partial(apply_kernel, group), out_shape=(shape,...]
where the time goes in v5:
time: 53.7 us; the launch traced here: 53.3 us
  Pallas kernels  52.6 us (98%)
  between operations  0.64 us (1%)
    pallas_call x1, Pallas kernels, main_call(): pl.pallas_call(functools.partial(main_kernel, count, cuts, rows), out_sha...  45.8 us
    pallas_call x1, Pallas kernels, apply_sinks(): pl.pallas_call(functools.partial(apply_kernel, group), out_shape=(shape,...  6.87 us

profile of v5, /device:TPU:7, one launch (start us, length us, event | category | flops | bytes accessed | tf_op | source)
XLA Modules:
  0.0 53.3 jit_solution(10807909161553468767)
XLA Ops:
  0.6 45.8 %project_sum_close.1 = (bf16[2,3,2,768,768]{4,3,2,1,0:T(8,128)(2,1)S(1)}, bf16[2,8,48,384]{3,2,1,0:T(8,128)(2,1)S(1)}) custom-call(s32[2,3]{1,0:T(2,128)} %mom_hbm.1, s32[2,4]{1,0:T(2,128)} %perm_hbm.3, s32[2,4]{1,0:T(2,128)} %sign_hbm.3, s32[2,16,128]{2,1,0:T(8,128)} %bitcast.9, bf16[2,3,192,4096]{3,2,1,0:T(8,128)(2,1)} %bitcast.7, ...), custom_call_target="tpu_custom_call" | custom-call | tf_op jit(solution)/shard_map/project_sum_close/pallas_call | solution.py:258
  46.4 6.9 %apply_sinks.1 = (bf16[2,2,1,768,768]{4,3,2,1,0:T(8,128)(2,1)}, bf16[2,2,1,768,768]{4,3,2,1,0:T(8,128)(2,1)}) custom-call(s32[2,4]{1,0:T(2,128)} %perm_hbm.3, s32[2,4]{1,0:T(2,128)} %sign_hbm.3, bf16[2,384,384]{2,1,0:T(8,128)(2,1)S(1)} %bitcast.6, bf16[2,3,2,768,768]{4,3,2,1,0:T(8,128)(2,1)S(1)} %get-tuple-element.5.x_ref), custom_call_target="tpu_custom_call" | custom-call | tf_op jit(solution)/shard_map/apply_sinks/pallas_call | solution.py:372

commit v6 on v5

--- a/solution.py
+++ b/solution.py
@@ -96,8 +96,7 @@
                 mixed[q, c, :, a * NEV : (a + 1) * NEV] = value[:, q * NEV : (q + 1) * NEV]
     keep = pl.ds(start, rows)
 
-    @pl.loop(0, 2)
-    def _(q):
+    for q in range(2):
         before(q)
         for left in range(0, NDIM, WIDTH):
             cols = slice(left, left + WIDTH)
@@ -128,12 +127,10 @@
         turn = lax.rem(i, depth)
         return pltpu.make_async_copy(vec_hbm.at[:, i // cuts, :, span], vecs.at[turn], vec_sem.at[turn])
 
+    fetch(0).start()
     for copy in small:
         copy.start()
-    for i in range(depth):
-        fetch(i).start()
     fetch_tau = pltpu.make_async_copy(tau_hbm, tau, tau_sem)
-    fetch_tau.start()
 
     slot = lax.rem(time, 2)
     sibling = {"ta": time + 1 - 2 * slot}
@@ -148,6 +145,9 @@
     small[1].wait()
     load_phases(mom_ref, site_ref, phase)
     fetch(0).wait()
+    for i in range(1, depth):
+        fetch(i).start()
+    fetch_tau.start()
     acc[...] = jnp.zeros_like(acc)
 
     @pl.loop(0, chunks)
@@ -232,10 +232,11 @@
     @pl.loop(0, last + 1)
     def _(i):
         def before(q):
-            @pl.when((i == last) & (q == 1))
-            def _():
-                sink.wait_recv()
-                onward.start()
+            if q == 1:
+                @pl.when(i == last)
+                def _():
+                    sink.wait_recv()
+                    onward.start()
 
         start = pl.multiple_of(lax.rem(i, blocks) * rows, rows)
         close_rows(i // blocks, start, rows, table, spins, moved, mixed, out_ref, before)

time: 53.7 us -> 53.9 us (level)
  no operation moved by 1% of the time
where the time goes in v6:
time: 53.9 us; the launch traced here: 53.4 us
  Pallas kernels  52.8 us (98%)
  between operations  0.64 us (1%)
    pallas_call x1, Pallas kernels, main_call(): pl.pallas_call(functools.partial(main_kernel, count, cuts, rows), out_sha...  45.9 us
    pallas_call x1, Pallas kernels, apply_sinks(): pl.pallas_call(functools.partial(apply_kernel, group), out_shape=(shape,...  6.87 us

profile of v6, /device:TPU:7, one launch (start us, length us, event | category | flops | bytes accessed | tf_op | source)
XLA Modules:
  0.0 53.4 jit_solution(5880854864559638233)
XLA Ops:
  0.6 45.9 %project_sum_close.1 = (bf16[2,3,2,768,768]{4,3,2,1,0:T(8,128)(2,1)S(1)}, bf16[2,8,48,384]{3,2,1,0:T(8,128)(2,1)S(1)}) custom-call(s32[2,3]{1,0:T(2,128)} %mom_hbm.1, s32[2,4]{1,0:T(2,128)} %perm_hbm.3, s32[2,4]{1,0:T(2,128)} %sign_hbm.3, s32[2,16,128]{2,1,0:T(8,128)} %bitcast.9, bf16[2,3,192,4096]{3,2,1,0:T(8,128)(2,1)} %bitcast.7, ...), custom_call_target="tpu_custom_call" | custom-call | tf_op jit(solution)/shard_map/project_sum_close/pallas_call | solution.py:259
  46.5 6.9 %apply_sinks.1 = (bf16[2,2,1,768,768]{4,3,2,1,0:T(8,128)(2,1)}, bf16[2,2,1,768,768]{4,3,2,1,0:T(8,128)(2,1)}) custom-call(s32[2,4]{1,0:T(2,128)} %perm_hbm.3, s32[2,4]{1,0:T(2,128)} %sign_hbm.3, bf16[2,384,384]{2,1,0:T(8,128)(2,1)S(1)} %bitcast.6, bf16[2,3,2,768,768]{4,3,2,1,0:T(8,128)(2,1)S(1)} %get-tuple-element.5.x_ref), custom_call_target="tpu_custom_call" | custom-call | tf_op jit(solution)/shard_map/apply_sinks/pallas_call | solution.py:373
